TPU v7x, 32 devices: a whole 2x2x4 slice. The times are simulated.
32 devices in a mesh: col: 4 (over z), row: 8 (over y, x, core).
Axes of the slice: x: 2, y: 2, z: 4, core: 2. Of those that a mesh axis runs over, the one named last changes fastest.
Arguments:
- w_gate: float32 [768, 2048], P('row', 'col')
- w_up: float32 [768, 2048], P('row', 'col')
- w_down: float32 [2048, 768], P('row', 'col')
- x_norm: bfloat16 [32768, 768], P(None, 'row')
- x_act: bfloat16 [32768, 2048], P(None, 'row')
- dy_gate: bfloat16 [32768, 2048], P(None, 'col')
- dy_up: bfloat16 [32768, 2048], P(None, 'col')
- dy_down: bfloat16 [32768, 768], P(None, 'col')
- r_gate: float32 [768], P('row')
- c_gate: float32 [2048], P('col')
- r_up: float32 [768], P('row')
- c_up: float32 [2048], P('col')
- r_down: float32 [2048], P('row')
- c_down: float32 [768], P('col')
- hyper_params: float32 [3], replicated
Outputs:
- output 1: float32 [768, 2048], P('row', 'col')
- output 2: float32 [768, 2048], P('row', 'col')
- output 3: float32 [2048, 768], P('row', 'col')
- output 4: float32 [768], P('row')
- output 5: float32 [2048], P('col')
- output 6: float32 [768], P('row')
- output 7: float32 [2048], P('col')
- output 8: float32 [2048], P('row')
- output 9: float32 [768], P('col')
- output 10: bfloat16 [32768, 768], P(None, 'row')
- output 11: bfloat16 [32768, 2048], P(None, 'row')
All inputs are finite; a program needn't handle non-finite values.
Results may differ from a plain program's by a relative error of at most 0.001.
Values are sent between devices in bfloat16 or wider.
A program may use at most 1 GiB of HBM per device.

v0:
```python
import jax
import jax.numpy as jnp
from jax import lax
from jax.sharding import PartitionSpec as P

EPS_ONE = 1e-30
EPS_TWO = 1e-3


def factored_step(w_loc, grad_loc, r_loc, c_loc, hyper_params, m_total, n_total):
    beta_two = hyper_params[0]
    grad_sq = grad_loc * grad_loc + EPS_ONE
    row_sum = lax.psum(jnp.sum(grad_sq, axis=1), 'col')
    col_sum = lax.psum(jnp.sum(grad_sq, axis=0), 'row')
    r_new = beta_two * r_loc + (1.0 - beta_two) * (row_sum / n_total)
    c_new = beta_two * c_loc + (1.0 - beta_two) * (col_sum / m_total)
    r_mean = lax.psum(jnp.sum(r_new), 'row') / m_total
    update = grad_loc * lax.rsqrt(r_new[:, None] * c_new[None, :] / r_mean)
    u_sq = lax.psum(jnp.sum(update * update), ('row', 'col'))
    rms_u = jnp.sqrt(u_sq / (m_total * n_total))
    update_hat = update / jnp.maximum(1.0, rms_u / hyper_params[2])
    w_sq = lax.psum(jnp.sum(w_loc * w_loc), ('row', 'col'))
    step_size = hyper_params[1] * jnp.maximum(EPS_TWO, jnp.sqrt(w_sq / (m_total * n_total)))
    return w_loc - step_size * update_hat, r_new, c_new


def weight_grad(activations, grad_out):
    return lax.dot_general(activations, grad_out, (((0,), (0,)), ((), ())), preferred_element_type=jnp.float32)


def input_grad(grad_out, weight):
    return lax.dot_general(grad_out, weight.astype(jnp.bfloat16), (((1,), (1,)), ((), ())), preferred_element_type=jnp.float32)


def solution(mesh):
    row_size = mesh.shape['row']
    col_size = mesh.shape['col']
    weight_spec = P('row', 'col')
    act_spec = P(None, 'row')
    grad_spec = P(None, 'col')
    in_specs = (weight_spec,) * 3 + (act_spec, act_spec) + (grad_spec,) * 3 + (P('row'), P('col')) * 3 + (P(),)
    out_specs = (weight_spec,) * 3 + (P('row'), P('col')) * 3 + (act_spec, act_spec)

    def body(w_gate, w_up, w_down, x_norm, x_act, dy_gate, dy_up, dy_down, r_gate, c_gate, r_up, c_up, r_down, c_down, hyper_params):
        d_model = w_gate.shape[0] * row_size
        d_ff = w_gate.shape[1] * col_size
        new_gate, r_gate_new, c_gate_new = factored_step(w_gate, weight_grad(x_norm, dy_gate), r_gate, c_gate, hyper_params, d_model, d_ff)
        new_up, r_up_new, c_up_new = factored_step(w_up, weight_grad(x_norm, dy_up), r_up, c_up, hyper_params, d_model, d_ff)
        new_down, r_down_new, c_down_new = factored_step(w_down, weight_grad(x_act, dy_down), r_down, c_down, hyper_params, d_ff, d_model)
        dx_norm = lax.psum(input_grad(dy_gate, w_gate) + input_grad(dy_up, w_up), 'col').astype(jnp.bfloat16)
        dx_act = lax.psum(input_grad(dy_down, w_down), 'col').astype(jnp.bfloat16)
        return (new_gate, new_up, new_down, r_gate_new, c_gate_new, r_up_new, c_up_new, r_down_new, c_down_new, dx_norm, dx_act)

    return jax.shard_map(body, mesh=mesh, in_specs=in_specs, out_specs=out_specs, check_vma=False)
```

profile of v0, /device:TPU:0, one launch (start us, length us, event | category | flops | bytes accessed | tf_op | source)
XLA Modules:
  0.0 1710.9 jit_solution(18267704092922864488)
XLA Ops:
  0.6 0.0 copy-start
  0.7 15.4 fusion.2
  16.1 0.0 copy-done
  16.1 13.8 fusion
  29.9 0.0 copy-start.1
  29.9 12.9 fusion.4
  42.8 0.0 copy-done.1
  42.8 0.0 copy-start.3
  42.8 20.3 %fusion.6 = f32[32768,256]{1,0:T(8,128)} fusion(bf16[32768,192]{0,1:T(8,128)(2,1)} %param.22, f32[256,192]{0,1:T(8,128)S(1)} %copy-done.1), kind=kOutput, calls=%fused_computation.22 | convolution fusion | flops 3221274624 | bytes 46333952 | tf_op jit(solution)/shard_map/dot_general | solution.py:32
  63.2 0.0 copy-done.3
  63.2 25.7 %fusion.9 = f32[32768,96]{0,1:T(8,128)} fusion(bf16[32768,512]{1,0:T(8,128)(2,1)} %param.20, f32[96,512]{1,0:T(8,128)S(1)} %copy-done.3), kind=kOutput, calls=%fused_computation.25 | convolution fusion | flops 3221274624 | bytes 46333952 | tf_op jit(solution)/shard_map/dot_general | solution.py:32
  88.9 0.0 copy-done.2
  88.9 23.0 %convolution_add_fusion = f32[32768,96]{0,1:T(8,128)} fusion(f32[32768,96]{0,1:T(8,128)} %fusion.9, bf16[32768,512]{1,0:T(8,128)(2,1)} %param.21, f32[96,512]{1,0:T(8,128)S(1)} %copy-done.2), kind=kOutput, calls=%fused_computation | convolution fusion | flops 3224420352 | bytes 58916864 | tf_op jit(solution)/shard_map/dot_general | solution.py:32
  111.8 0.0 copy-start.13
  111.8 0.0 copy-start.14
  111.9 0.0 copy-start.11
  111.9 0.0 copy-start.12
  111.9 1526.1 %all-reduce.4 = (f32[96]{0:T(128)S(1)}, f32[96]{0:T(128)S(1)}, f32[256]{0:T(256)S(1)}, bf16[32768,96]{0,1:T(8,128)(2,1)}, bf16[32768,256]{1,0:T(8,128)(2,1)}) all-reduce(f32[96]{0:T(128)S(1)} %get-tuple-element.16, f32[96]{0:T(128)S(1)} %get-tuple-element.14, f32[256]{0:T(256)S(1)} %get-tuple-element.12, ...), channel_id=1, replica_groups=mesh['col'=4,'row'=8] {'col'}, use_global_device_ids=true, to_apply=%region_3.0 | all-reduce | flops 11534784 | bytes 69209600 | tf_op jit(solution)/shard_map/psum | solution.py:13
  1638.0 0.0 copy-done.10
  1638.0 0.7 fusion.14
  1639.3 0.0 copy-done.15
  1639.3 0.0 copy-done.16
  1639.3 1.2 fusion.12
  1640.6 0.0 copy-done.13
  1640.6 1.2 fusion.11
  1641.9 12.7 all-reduce.1
  1654.6 0.0 copy-done.14
  1654.6 0.6 multiply_add_fusion.5
  1655.2 0.0 copy-start.7
  1655.9 0.7 multiply_reduce_fusion
  1656.6 0.0 copy-done.11
  1656.6 0.6 multiply_add_fusion.3
  1657.3 0.0 copy-start.4
  1657.9 0.8 multiply_reduce_fusion.2
  1658.6 0.0 copy-done.12
  1658.6 0.6 multiply_add_fusion.4
  1659.3 0.0 copy-start.5
  1660.0 0.7 multiply_reduce_fusion.4
  1660.7 0.6 multiply_reduce_fusion.3
  1661.4 0.6 multiply_reduce_fusion.1
  1662.0 38.2 %all-reduce = (f32[]{:T(128)}, f32[]{:T(128)}, f32[]{:T(128)}, f32[]{:T(128)}, f32[]{:T(128)}, /*index=5*/f32[]{:T(128)}) all-reduce(f32[]{:T(128)} %multiply_reduce_fusion.4, f32[]{:T(128)} %get-tuple-element.49, f32[]{:T(128)} %multiply_reduce_fusion.2, f32[]{:T(128)} %get-tuple-element.48, ...), channel_id=1, replica_groups=mesh['col'=4,'row'=8] {'row','col'}, use_global_device_ids=true, to_apply=%region_9.0 | all-reduce | flops 6 | bytes 48 | tf_op jit(solution)/shard_map/psum | solution.py:19
  1702.8 0.8 multiply_subtract_fusion
  1706.4 0.8 multiply_subtract_fusion.1
  1709.9 0.8 multiply_subtract_fusion.2
  1710.7 0.0 copy-done.8
  1710.7 0.0 copy-done.9
  1710.7 0.0 copy-done.6
  1710.7 0.0 copy-done.7
  (9 shorter events, 0.0 us)
Async XLA Ops:
  0.6 15.4 copy-start
  29.9 12.9 copy-start.1
  42.8 20.4 %copy-start.3 = (f32[96,512]{1,0:T(8,128)S(1)}, f32[96,512]{1,0:T(8,128)}, u32[]{:S(2)}) copy-start(f32[96,512]{1,0:T(8,128)} %param.15) | copy-start | bytes 589828
  63.2 25.7 %copy-start.2 = (f32[96,512]{1,0:T(8,128)S(1)}, f32[96,512]{1,0:T(8,128)}, u32[]{:S(2)}) copy-start(f32[96,512]{1,0:T(8,128)} %param.16) | copy-start | bytes 589828
  111.8 1526.2 %copy-start.10 = (f32[3]{0:T(128)S(1)}, f32[3]{0:T(128)}, u32[]{:S(2)}) copy-start(f32[3]{0:T(128)} %param.29) | copy-start | bytes 40
  111.8 1527.5 %copy-start.15 = (f32[96]{0:T(128)S(1)}, f32[96]{0:T(128)}, u32[]{:S(2)}) copy-start(f32[96]{0:T(128)} %param.25) | copy-start | bytes 1156
  111.8 1527.5 %copy-start.16 = (f32[96]{0:T(128)S(1)}, f32[96]{0:T(128)}, u32[]{:S(2)}) copy-start(f32[96]{0:T(128)} %param.23) | copy-start | bytes 1156
  111.8 1528.8 %copy-start.13 = (f32[256]{0:T(256)S(1)}, f32[256]{0:T(256)}, u32[]{:S(2)}) copy-start(f32[256]{0:T(256)} %param.27) | copy-start | bytes 3076
  111.8 1542.7 %copy-start.14 = (f32[192]{0:T(256)S(1)}, f32[192]{0:T(256)}, u32[]{:S(2)}) copy-start(f32[192]{0:T(256)} %param.28) | copy-start | bytes 2308
  111.9 1544.8 %copy-start.11 = (f32[512]{0:T(512)S(1)}, f32[512]{0:T(512)}, u32[]{:S(2)}) copy-start(f32[512]{0:T(512)} %param.26) | copy-start | bytes 6148
  111.9 1546.8 %copy-start.12 = (f32[512]{0:T(512)S(1)}, f32[512]{0:T(512)}, u32[]{:S(2)}) copy-start(f32[512]{0:T(512)} %param.24) | copy-start | bytes 6148
  1640.6 70.1 %copy-start.8 = (f32[96]{0:T(128)}, f32[96]{0:T(128)S(1)}, u32[]{:S(2)}) copy-start(f32[96]{0:T(128)S(1)} %get-tuple-element.37) | copy-start | bytes 1156
  1640.6 70.1 %copy-start.9 = (f32[96]{0:T(128)}, f32[96]{0:T(128)S(1)}, u32[]{:S(2)}) copy-start(f32[96]{0:T(128)S(1)} %get-tuple-element.47) | copy-start | bytes 1156
  1641.9 68.8 %copy-start.6 = (f32[256]{0:T(256)}, f32[256]{0:T(256)S(1)}, u32[]{:S(2)}) copy-start(f32[256]{0:T(256)S(1)} %get-tuple-element.35) | copy-start | bytes 3076
  1655.2 55.4 %copy-start.7 = (f32[192]{0:T(256)}, f32[192]{0:T(256)S(1)}, u32[]{:S(2)}) copy-start(f32[192]{0:T(256)S(1)} %multiply_add_fusion.5) | copy-start | bytes 2308
  1657.3 53.4 %copy-start.4 = (f32[512]{0:T(512)}, f32[512]{0:T(512)S(1)}, u32[]{:S(2)}) copy-start(f32[512]{0:T(512)S(1)} %multiply_add_fusion.3) | copy-start | bytes 6148
  1659.3 51.4 %copy-start.5 = (f32[512]{0:T(512)}, f32[512]{0:T(512)S(1)}, u32[]{:S(2)}) copy-start(f32[512]{0:T(512)S(1)} %multiply_add_fusion.4) | copy-start | bytes 6148
where the time goes:
time: 1710 us
  blocking collectives  1580 us (92%)
  matrix products  111 us (6%)
    psum x1, blocking collectives, factored_step(): row_sum = lax.psum(jnp.sum(grad_sq, axis=1), 'col')  1530 us
    dot_general x3, matrix products, input_grad(): lax.dot_general(grad_out, weight.astype(jnp.bfloat16), (((1,), (1,)), (()...  69 us
    dot_general x3, matrix products, weight_grad(): lax.dot_general(activations, grad_out, (((0,), (0,)), ((), ())), preferre...  42.1 us
    psum x1, blocking collectives, factored_step(): u_sq = lax.psum(jnp.sum(update * update), ('row', 'col'))  38.2 us

commit v1 on v0

v1 whole, which is shorter than its diff:
```python
import functools

import jax
import jax.numpy as jnp
from jax import lax
from jax.experimental import pallas as pl
from jax.experimental.pallas import tpu as pltpu
from jax.sharding import PartitionSpec as P

EPS_ONE = 1e-30
EPS_TWO = 1e-3
CHUNKS = 16
NZ = 4
NR = 8
HOME_LAG = (3, 2, 2, 3)
F32 = jnp.float32
BF16 = jnp.bfloat16


def mm(a, b):
    return lax.dot_general(a, b, (((1,), (0,)), ((), ())), preferred_element_type=F32)


def mm_nt(a, b):
    return lax.dot_general(a, b, (((1,), (1,)), ((), ())), preferred_element_type=F32)


def mm_tn(a, b):
    return lax.dot_general(a, b, (((0,), (0,)), ((), ())), preferred_element_type=F32)


def kernel(
    xt, xa, dyg, dyu, dydt, wg, wu, wdt,
    outt, oact, gg, gu, gdt,
    rsu, rsd, ag, dz, dxy, wall, part, txt, txa, tg, tu, td, dloc, st,
    tile_sem, dloc_sem, rsu_r, rsd_r, ag_r, dz_r, dxy_r, w_r, wp_r,
    rsu_s, rsd_s, agu_s, agd_s, dzu_s, dzd_s, dxy_s, w_s, wp_s, wl_s,
    out_sem, st_l, st_s, oact_r,
):
    z = lax.axis_index("col")
    i = lax.axis_index("row")
    core = i % 2
    xx = (i // 2) % 2
    yy = i // 4
    base = z * NR
    partner = i + 1 - 2 * core
    xn = i + 2 * (1 - 2 * xx)
    yn = i + 4 * (1 - 2 * yy)
    dg = xn + 4 * (1 - 2 * yy)
    plane_peers = (xn, yn, dg)
    C = rsu.shape[1]
    S = rsu.shape[3]
    Sd = dz.shape[3]
    T = xa.shape[0]
    home_len = T // NZ
    eighth = T // NR
    up_id = base + NR + i
    dn_id = base - NR + i

    def rcopy(src, dst, ssem, rsem, dev):
        return pltpu.make_async_remote_copy(
            src, dst, ssem, rsem, device_id=dev, device_id_type=pl.DeviceIdType.LOGICAL
        )

    barrier = pltpu.get_barrier_semaphore()
    peers = [base + q for q in plane_peers] + [base + partner]
    peers += [((z + d) % NZ) * NR + i for d in (1, 2, 3)]
    for dev in peers:
        pl.semaphore_signal(barrier, inc=1, device_id=dev, device_id_type=pl.DeviceIdType.LOGICAL)

    def order(j):
        odd = j % 2
        return (1 - odd) * (3 - j // 2) + odd * (j // 2)

    def tile_at(k, j):
        h = order(j)
        lag = jnp.where(h > z, z, jnp.where(h < z, NZ - 1 - z, jnp.maximum(z, NZ - 1 - z)))
        c = k - lag
        return h, c, jnp.logical_and(c >= 0, c < C)

    def tile_copies(h, c, slot):
        t0 = pl.multiple_of(h * home_len + c * S, S)
        rows = pl.ds(t0, S)
        return [
            pltpu.make_async_copy(xt.at[:, rows], txt.at[slot], tile_sem.at[slot, 0]),
            pltpu.make_async_copy(xa.at[rows, :], txa.at[slot], tile_sem.at[slot, 1]),
            pltpu.make_async_copy(dyg.at[rows, :], tg.at[slot], tile_sem.at[slot, 2]),
            pltpu.make_async_copy(dyu.at[rows, :], tu.at[slot], tile_sem.at[slot, 3]),
            pltpu.make_async_copy(dydt.at[:, rows], td.at[slot], tile_sem.at[slot, 4]),
        ]

    def start_tile(k, j, slot):
        h, c, on = tile_at(k, j)

        @pl.when(on)
        def _():
            for cp in tile_copies(h, c, slot):
                cp.start()

    def dloc_copies(c, slot):
        return [
            pltpu.make_async_copy(
                dydt.at[:, pl.ds(pl.multiple_of(q * eighth + c * Sd, Sd), Sd)],
                dloc.at[slot, s], dloc_sem.at[slot, s])
            for s, q in enumerate((i,) + plane_peers)
        ]

    def st_local(c, slot):
        return [
            pltpu.make_async_copy(
                st.at[slot, 0, s],
                oact.at[pl.ds(pl.multiple_of(q * eighth + c * Sd, Sd), Sd), :],
                st_l.at[slot, s])
            for s, q in enumerate((i,) + plane_peers)
        ]

    def st_remote(c, slot):
        return [
            rcopy(
                st.at[slot, 1, s],
                oact.at[pl.ds(pl.multiple_of(q * eighth + c * Sd, Sd), Sd), :],
                st_s.at[slot, s], oact_r.at[0], base + partner)
            for s, q in enumerate((i,) + plane_peers)
        ]

    def out_copy(h, c):
        return pltpu.make_async_copy(
            ag.at[h, c], outt.at[:, pl.ds(pl.multiple_of(h * home_len + c * S, S), S)], out_sem.at[0])

    def w_copy(d):
        return rcopy(wdt, wall.at[0, NZ - d], w_s.at[d - 1], w_r.at[NZ - d - 1], ((z + d) % NZ) * NR + i)

    wp_copy = rcopy(wall.at[0], wall.at[1], wp_s.at[0], wp_r.at[0], base + partner)

    start_tile(0, 0, 0)
    gg[...] = jnp.zeros_like(gg)
    gu[...] = jnp.zeros_like(gu)
    gdt[...] = jnp.zeros_like(gdt)
    wl = pltpu.make_async_copy(wdt, wall.at[0, 0], wl_s.at[0])
    wl.start()
    wl.wait()
    pl.semaphore_wait(barrier, len(peers))
    for d in (1, 2, 3):
        w_copy(d).start()

    def step(k, carry):
        @pl.when(k < C)
        def _():
            src = dydt.at[:, pl.ds(pl.multiple_of(i * eighth + k * Sd, Sd), Sd)]

            @pl.when(z < NZ - 1)
            def _():
                rcopy(src, dz.at[k, 2], dzu_s.at[0], dz_r.at[2, k], up_id).start()

            @pl.when(z > 0)
            def _():
                rcopy(src, dz.at[k, 0], dzd_s.at[0], dz_r.at[0, k], dn_id).start()

        for d in (1, 2, 3):
            c = k - d
            ok = jnp.logical_and(c >= 0, c < C)

            @pl.when(jnp.logical_and(ok, z >= d))
            def _():
                rcopy(dz.at[c, 3 - d], dz.at[c, 3 - d], dzu_s.at[0], dz_r.at[3 - d, c], up_id).wait_recv()
                if d < 3:
                    @pl.when(z < NZ - 1)
                    def _():
                        rcopy(dz.at[c, 3 - d], dz.at[c, 2 - d], dzu_s.at[d], dz_r.at[2 - d, c], up_id).start()

            @pl.when(jnp.logical_and(ok, NZ - 1 - z >= d))
            def _():
                rcopy(dz.at[c, d - 1], dz.at[c, d - 1], dzd_s.at[0], dz_r.at[d - 1, c], dn_id).wait_recv()
                if d < 3:
                    @pl.when(z > 0)
                    def _():
                        rcopy(dz.at[c, d - 1], dz.at[c, d], dzd_s.at[d], dz_r.at[d, c], dn_id).start()

        cx = k - 3

        @pl.when(jnp.logical_and(cx >= 0, cx < C))
        def _():
            for s, q in enumerate(plane_peers):
                rcopy(dz.at[cx], dxy.at[s, cx], dxy_s.at[s], dxy_r.at[s, cx], base + q).start()

        for h in range(NZ):
            dist = jnp.abs(z - h)
            c = k - HOME_LAG[h] - dist

            @pl.when(jnp.logical_and(jnp.logical_and(c >= 0, c < C), z != h))
            def _():
                rcopy(ag.at[h, c], ag.at[h, c], agu_s.at[h], ag_r.at[h, c], up_id).wait_recv()

                if h < NZ - 2:
                    @pl.when(jnp.logical_and(z > h, z < NZ - 1))
                    def _():
                        rcopy(ag.at[h, c], ag.at[h, c], agu_s.at[h], ag_r.at[h, c], up_id).start()

                if h > 1:
                    @pl.when(jnp.logical_and(z < h, z > 0))
                    def _():
                        rcopy(ag.at[h, c], ag.at[h, c], agd_s.at[h], ag_r.at[h, c], dn_id).start()

                out_copy(h, c).start()

        def tile(j, carry2):
            slot = j % 2
            nj = j + 1
            start_tile(k + nj // 4, nj % 4, nj % 2)
            h, c, on = tile_at(k, j)

            @pl.when(on)
            def _():
                for cp in tile_copies(h, c, slot):
                    cp.wait()
                g = tg[slot]
                u = tu[slot]
                part[...] = mm_nt(wg[...], g) + mm_nt(wu[...], u)

                @pl.when(h > z)
                def _():
                    @pl.when(z > 0)
                    def _():
                        rcopy(rsu.at[h - 1, c], rsu.at[h - 1, c], rsu_s.at[h - 1], rsu_r.at[h - 1, c], up_id).wait_recv()
                        rsu[h - 1, c] = rsu[h - 1, c] + part[...]

                    @pl.when(z == 0)
                    def _():
                        rsu[h - 1, c] = part[...]

                    rcopy(rsu.at[h - 1, c], rsu.at[h - 1, c], rsu_s.at[h - 1], rsu_r.at[h - 1, c], up_id).start()

                @pl.when(h < z)
                def _():
                    @pl.when(z < NZ - 1)
                    def _():
                        rcopy(rsd.at[h, c], rsd.at[h, c], rsd_s.at[h], rsd_r.at[h, c], dn_id).wait_recv()
                        rsd[h, c] = rsd[h, c] + part[...]

                    @pl.when(z == NZ - 1)
                    def _():
                        rsd[h, c] = part[...]

                    rcopy(rsd.at[h, c], rsd.at[h, c], rsd_s.at[h], rsd_r.at[h, c], dn_id).start()

                @pl.when(h == z)
                def _():
                    @pl.when(z > 0)
                    def _():
                        rcopy(rsu.at[h - 1, c], rsu.at[h - 1, c], rsu_s.at[h - 1], rsu_r.at[h - 1, c], up_id).wait_recv()
                        part[...] = part[...] + rsu[h - 1, c]

                    @pl.when(z < NZ - 1)
                    def _():
                        rcopy(rsd.at[h, c], rsd.at[h, c], rsd_s.at[h], rsd_r.at[h, c], dn_id).wait_recv()
                        part[...] = part[...] + rsd[h, c]

                    ag[h, c] = part[...].astype(BF16)

                    @pl.when(z < NZ - 1)
                    def _():
                        rcopy(ag.at[h, c], ag.at[h, c], agu_s.at[h], ag_r.at[h, c], up_id).start()

                    @pl.when(z > 0)
                    def _():
                        rcopy(ag.at[h, c], ag.at[h, c], agd_s.at[h], ag_r.at[h, c], dn_id).start()

                    out_copy(h, c).start()

                gg[...] += mm(txt[slot], g)
                gu[...] += mm(txt[slot], u)
                gdt[...] += mm(td[slot], txa[slot])

            return carry2

        lax.fori_loop(0, 4, tile, 0)

        @pl.when(k == 1)
        def _():
            for d in (1, 2, 3):
                w_copy(NZ - d).wait_send()
                rcopy(wdt, wall.at[0, d], w_s.at[d - 1], w_r.at[d - 1], up_id).wait_recv()
            wp_copy.start()

        @pl.when(k == 3)
        def _():
            wp_copy.wait()

        cf = k - 4

        @pl.when(jnp.logical_and(cf >= 0, cf < C))
        def _():
            for cp in dloc_copies(cf, cf % 2):
                cp.start()

        ca = k - 5
        slot_a = ca % 2

        @pl.when(jnp.logical_and(ca >= 0, ca < C))
        def _():
            @pl.when(ca >= 2)
            def _():
                for cp in st_local(ca - 2, slot_a):
                    cp.wait()
                for cp in st_remote(ca - 2, slot_a):
                    cp.wait_send()

            locs = dloc_copies(ca, slot_a)
            outl = st_local(ca, slot_a)
            outr = st_remote(ca, slot_a)
            for s in range(4):
                locs[s].wait()
                if s == 0:
                    far = dz[ca]
                else:
                    rcopy(dz.at[ca], dxy.at[s - 1, ca], dxy_s.at[s - 1], dxy_r.at[s - 1, ca], base + xn).wait_recv()
                    far = dxy[s - 1, ca]
                lhs = jnp.concatenate([dloc[slot_a, s], far.reshape(3 * far.shape[1], Sd)], axis=0)
                for b in range(2):
                    w = wall[b].reshape(lhs.shape[0], wall.shape[3])
                    st[slot_a, b, s] = mm_tn(lhs, w).astype(BF16)
                outl[s].start()
                outr[s].start()

        return carry

    lax.fori_loop(0, C + 6, step, 0)

    for c in (C - 2, C - 1):
        for cp in st_local(c, c % 2):
            cp.wait()
        for cp in st_remote(c, c % 2):
            cp.wait_send()
    half = oact.at[pl.ds(0, T // 2), :]
    rcopy(half, half, st_s.at[0, 0], oact_r.at[0], base + partner).wait_recv()
    pltpu.make_async_copy(outt, outt, out_sem.at[0]).wait()
    for h in (1, 2, 3):
        @pl.when(h > z)
        def _():
            rcopy(rsu.at[h - 1], rsu.at[h - 1], rsu_s.at[h - 1], rsu_r.at[h - 1, 0], up_id).wait_send()
    for h in (0, 1, 2):
        @pl.when(h < z)
        def _():
            rcopy(rsd.at[h], rsd.at[h], rsd_s.at[h], rsd_r.at[h, 0], dn_id).wait_send()
    for h in range(NZ):
        if h < NZ - 1:
            @pl.when(jnp.logical_and(z >= h, z < NZ - 1))
            def _():
                rcopy(ag.at[h], ag.at[h], agu_s.at[h], ag_r.at[h, 0], up_id).wait_send()
        if h > 0:
            @pl.when(jnp.logical_and(z <= h, z > 0))
            def _():
                rcopy(ag.at[h], ag.at[h], agd_s.at[h], ag_r.at[h, 0], dn_id).wait_send()
    dzall = dxy.at[0, :, 0]
    for d in range(3):
        @pl.when(jnp.logical_and(z >= d, z < NZ - 1))
        def _():
            rcopy(dzall, dzall, dzu_s.at[d], dz_r.at[0, 0], up_id).wait_send()

        @pl.when(jnp.logical_and(NZ - 1 - z >= d, z > 0))
        def _():
            rcopy(dzall, dzall, dzd_s.at[d], dz_r.at[0, 0], dn_id).wait_send()
    for s in range(3):
        rcopy(dz, dxy.at[s], dxy_s.at[s], dxy_r.at[s, 0], base + xn).wait_send()


def main_call(xt, xa, dyg, dyu, dydt, wg, wu, wdt):
    T, ka = xa.shape
    m = xt.shape[0]
    n = dyg.shape[1]
    nd = dydt.shape[0]
    C = CHUNKS
    S = T // NZ // C
    Sd = T // NR // C
    dma = pltpu.SemaphoreType.DMA
    anyspec = pl.BlockSpec(memory_space=pl.ANY)
    vspec = pl.BlockSpec(memory_space=pltpu.VMEM)
    scratch = [
        pltpu.VMEM((3, C, m, S), F32),
        pltpu.VMEM((3, C, m, S), F32),
        pltpu.VMEM((NZ, C, m, S), BF16),
        pltpu.VMEM((C, 3, nd, Sd), BF16),
        pltpu.VMEM((3, C, 3, nd, Sd), BF16),
        pltpu.VMEM((2, NZ, nd, ka), BF16),
        pltpu.VMEM((m, S), F32),
        pltpu.VMEM((2, m, S), BF16),
        pltpu.VMEM((2, S, ka), BF16),
        pltpu.VMEM((2, S, n), BF16),
        pltpu.VMEM((2, S, n), BF16),
        pltpu.VMEM((2, nd, S), BF16),
        pltpu.VMEM((2, 4, nd, Sd), BF16),
        pltpu.VMEM((2, 2, 4, Sd, ka), BF16),
        dma((2, 5)), dma((2, 4)),
        dma((3, C)), dma((3, C)), dma((NZ, C)), dma((3, C)), dma((3, C)), dma((3,)), dma((1,)),
        dma((3,)), dma((3,)), dma((NZ,)), dma((NZ,)), dma((3,)), dma((3,)), dma((3,)), dma((3,)), dma((1,)), dma((1,)),
        dma((1,)), dma((2, 4)), dma((2, 4)), dma((1,)),
    ]
    return pl.pallas_call(
        kernel,
        out_shape=(
            jax.ShapeDtypeStruct((m, T), BF16),
            jax.ShapeDtypeStruct((T, ka), BF16),
            jax.ShapeDtypeStruct((m, n), F32),
            jax.ShapeDtypeStruct((m, n), F32),
            jax.ShapeDtypeStruct((nd, ka), F32),
        ),
        in_specs=[anyspec] * 5 + [vspec] * 3,
        out_specs=(anyspec, anyspec, vspec, vspec, vspec),
        scratch_shapes=scratch,
        compiler_params=pltpu.CompilerParams(
            collective_id=0, has_side_effects=True, vmem_limit_bytes=67_000_000),
    )(xt, xa, dyg, dyu, dydt, wg, wu, wdt)


def factored_step(w_loc, grad_loc, r_loc, c_loc, hyper_params, m_total, n_total):
    beta_two = hyper_params[0]
    grad_sq = grad_loc * grad_loc + EPS_ONE
    row_sum = lax.psum(jnp.sum(grad_sq, axis=1), 'col')
    col_sum = lax.psum(jnp.sum(grad_sq, axis=0), 'row')
    r_new = beta_two * r_loc + (1.0 - beta_two) * (row_sum / n_total)
    c_new = beta_two * c_loc + (1.0 - beta_two) * (col_sum / m_total)
    r_mean = lax.psum(jnp.sum(r_new), 'row') / m_total
    update = grad_loc * lax.rsqrt(r_new[:, None] * c_new[None, :] / r_mean)
    u_sq = lax.psum(jnp.sum(update * update), ('row', 'col'))
    rms_u = jnp.sqrt(u_sq / (m_total * n_total))
    update_hat = update / jnp.maximum(1.0, rms_u / hyper_params[2])
    w_sq = lax.psum(jnp.sum(w_loc * w_loc), ('row', 'col'))
    step_size = hyper_params[1] * jnp.maximum(EPS_TWO, jnp.sqrt(w_sq / (m_total * n_total)))
    return w_loc - step_size * update_hat, r_new, c_new


def solution(mesh):
    row_size = mesh.shape['row']
    col_size = mesh.shape['col']
    weight_spec = P('row', 'col')
    act_spec = P(None, 'row')
    grad_spec = P(None, 'col')
    in_specs = (weight_spec,) * 3 + (act_spec, act_spec) + (grad_spec,) * 3 + (P('row'), P('col')) * 3 + (P(),)
    out_specs = (weight_spec,) * 3 + (P('row'), P('col')) * 3 + (act_spec, act_spec)

    def body(w_gate, w_up, w_down, x_norm, x_act, dy_gate, dy_up, dy_down, r_gate, c_gate, r_up, c_up, r_down, c_down, hyper_params):
        d_model = w_gate.shape[0] * row_size
        d_ff = w_gate.shape[1] * col_size
        outt, dx_act, g_gate, g_up, g_down_t = main_call(
            x_norm.T, x_act, dy_gate, dy_up, dy_down.T,
            w_gate.astype(BF16), w_up.astype(BF16), w_down.T.astype(BF16))
        new_gate, r_gate_new, c_gate_new = factored_step(w_gate, g_gate, r_gate, c_gate, hyper_params, d_model, d_ff)
        new_up, r_up_new, c_up_new = factored_step(w_up, g_up, r_up, c_up, hyper_params, d_model, d_ff)
        new_down, r_down_new, c_down_new = factored_step(w_down, g_down_t.T, r_down, c_down, hyper_params, d_ff, d_model)
        return (new_gate, new_up, new_down, r_gate_new, c_gate_new, r_up_new, c_up_new, r_down_new, c_down_new, outt.T, dx_act)

    return jax.shard_map(body, mesh=mesh, in_specs=in_specs, out_specs=out_specs, check_vma=False)
```

time: 1710 us -> 432 us (0.25)
  blocking collectives: 1580 us -> 61.2 us
  Pallas kernels: 0 us -> 312 us
  matrix products: 111 us -> 0 us
  local copies, waits for them, and re-layouts: 0.75 us -> 21.1 us
    psum x1, blocking collectives: 1530 us -> 10.4 us  [factored_step(): row_sum = lax.psum(jnp.sum(grad_sq, axis=1), 'col')]
    pallas_call x0 -> x1, Pallas kernels: none -> 312 us  [main_call(): pl.pallas_call(kernel, out_shape=(jax.ShapeDtypeStruct((m, T), BF16), jax...]
    dot_general x6 -> x0, matrix products: 111 us -> none  [the longest x3 69 us: input_grad(): lax.dot_general(grad_out, weight.astype(jnp.bfloat16), (((1,), (1,)), (()...]
    unnamed x34 -> x26, local copies, waits for them, and re-layouts: 0.09 us -> 19.7 us
where the time goes in v1:
time: 432 us; the launch traced here: 430 us
  Pallas kernels  312 us (72%)
  blocking collectives  61.2 us (14%)
  other arithmetic  24.7 us (6%)
  local copies, waits for them, and re-layouts  21.1 us (5%)
  between operations  11.2 us (3%)
    pallas_call x1, Pallas kernels, main_call(): pl.pallas_call(kernel, out_shape=(jax.ShapeDtypeStruct((m, T), BF16), jax...  312 us
    psum x1, blocking collectives, factored_step(): u_sq = lax.psum(jnp.sum(update * update), ('row', 'col'))  38 us
    unnamed x26, local copies, waits for them, and re-layouts  19.7 us
    psum x1, blocking collectives, factored_step(): r_mean = lax.psum(jnp.sum(r_new), 'row') / m_total  12.7 us
    psum x1, blocking collectives, factored_step(): row_sum = lax.psum(jnp.sum(grad_sq, axis=1), 'col')  10.4 us

profile of v1, /device:TPU:0, one launch (start us, length us, event | category | flops | bytes accessed | tf_op | source)
XLA Modules:
  0.0 430.0 jit_solution(17464235172974166)
XLA Ops:
  0.6 1.4 fusion.10
  2.7 2.3 multiply_reduce_fusion.5
  4.9 2.3 multiply_reduce_fusion.3
  7.2 2.3 multiply_reduce_fusion.1
  9.5 0.0 copy-start.10
  9.5 0.0 copy-start.11
  9.5 0.0 copy-start.8
  9.5 0.0 copy-start.6
  9.5 0.0 copy-start.9
  9.5 0.0 copy-start.7
  9.5 311.9 %shard_map.230 = (bf16[96,32768]{1,0:T(8,128)(2,1)}, bf16[32768,256]{1,0:T(8,128)(2,1)}, f32[96,512]{1,0:T(8,128)}, f32[96,512]{1,0:T(8,128)}, f32[192,256]{1,0:T(8,128)}) custom-call(bf16[96,32768]{1,0:T(8,128)(2,1)} %bitcast.22, bf16[32768,256]{1,0:T(8,128)(2,1)} %xa.1, bf16[32768,512]{1,0:T(8,128)(2,1)} %dyg.1, bf16[32768,512]{1,0:T(8,128)(2,1)} %dyu.1, ...), custom_call_target="tpu_custom_call" | custom-call | tf_op jit(solution)/shard_map/pallas_call | solution.py:398
  321.4 1.1 fusion.5
  322.5 1.1 fusion.1
  323.6 1.1 fusion.3
  324.7 10.4 %all-reduce.2 = (f32[96]{0:T(128)S(1)}, f32[96]{0:T(128)S(1)}, f32[256]{0:T(256)S(1)}) all-reduce(f32[96]{0:T(128)S(1)} %get-tuple-element.26, f32[96]{0:T(128)S(1)} %get-tuple-element.24, f32[256]{0:T(256)S(1)} %get-tuple-element.22), channel_id=1, replica_groups=mesh['col'=4,'row'=8] {'col'}, use_global_device_ids=true, to_apply=%region_3.0 | all-reduce | flops 448 | bytes 3584 | tf_op jit(solution)/shard_map/psum | solution.py:418
  335.1 0.0 copy-done.10
  335.1 1.2 fusion.9
  336.3 0.0 copy-start.4
  336.3 0.0 copy-done.11
  336.3 1.2 fusion.8
  337.6 0.0 copy-start.5
  337.6 0.0 copy-done.8
  337.6 1.2 fusion.7
  338.8 0.0 copy-start.2
  338.8 12.7 %all-reduce.1 = (f32[]{:T(128)}, f32[512]{0:T(512)S(1)}, f32[]{:T(128)}, f32[512]{0:T(512)S(1)}, f32[]{:T(128)}, /*index=5*/f32[192]{0:T(256)S(1)}) all-reduce(f32[]{:T(128)} %get-tuple-element.46, f32[512]{0:T(512)S(1)} %get-tuple-element.25, f32[]{:T(128)} %get-tuple-element.44, ...), channel_id=1, replica_groups=mesh['col'=4,'row'=8] {'row'}, use_global_device_ids=true, to_apply=%region_7.0 | all-reduce | flops 1219 | bytes 9752 | tf_op jit(solution)/shard_map/psum | solution.py:422
  353.5 0.0 copy-done.6
  353.5 0.7 multiply_add_fusion.3
  354.2 0.0 copy-start
  354.2 1.7 multiply_reduce_fusion.4
  355.9 0.0 copy-done.9
  355.9 0.6 multiply_add_fusion.4
  356.5 0.0 copy-start.3
  356.5 1.7 multiply_reduce_fusion
  358.2 0.0 copy-done.7
  358.2 0.6 multiply_add_fusion.2
  358.8 0.0 copy-start.1
  358.9 1.7 multiply_reduce_fusion.2
  360.5 38.0 %all-reduce = (f32[]{:T(128)}, f32[]{:T(128)}, f32[]{:T(128)}, f32[]{:T(128)}, f32[]{:T(128)}, /*index=5*/f32[]{:T(128)}) all-reduce(f32[]{:T(128)} %multiply_reduce_fusion.4, f32[]{:T(128)} %get-tuple-element.52, f32[]{:T(128)} %multiply_reduce_fusion.2, f32[]{:T(128)} %get-tuple-element.50, ...), channel_id=1, replica_groups=mesh['col'=4,'row'=8] {'row','col'}, use_global_device_ids=true, to_apply=%region_9.0 | all-reduce | flops 6 | bytes 48 | tf_op jit(solution)/shard_map/psum | solution.py:424
  406.4 2.1 multiply_subtract_fusion.1
  408.5 1.8 multiply_subtract_fusion
  410.3 5.9 %copy.28 = bf16[32768,96]{0,1:T(8,128)(2,1)} copy(bf16[32768,96]{0,1:T(8,128)(2,1)} %bitcast.23) | data formatting | bytes 12582912
  416.2 13.8 %copy.29 = bf16[32768,256]{1,0:T(8,128)(2,1)} copy(bf16[32768,256]{1,0:T(8,128)(2,1)} %get-tuple-element.80) | data formatting | bytes 33554432
  430.0 0.0 copy-done.4
  430.0 0.0 copy-done.5
  430.0 0.0 copy-done.2
  430.0 0.0 copy-done
  430.0 0.0 copy-done.3
  430.0 0.0 copy-done.1
Async XLA Ops:
  9.5 325.6 %copy-start.10 = (f32[96]{0:T(128)S(1)}, f32[96]{0:T(128)}, u32[]{:S(2)}) copy-start(f32[96]{0:T(128)} %param.23) | copy-start | bytes 1156
  9.5 326.8 %copy-start.11 = (f32[96]{0:T(128)S(1)}, f32[96]{0:T(128)}, u32[]{:S(2)}) copy-start(f32[96]{0:T(128)} %param.25) | copy-start | bytes 1156
  9.5 328.1 %copy-start.8 = (f32[256]{0:T(256)S(1)}, f32[256]{0:T(256)}, u32[]{:S(2)}) copy-start(f32[256]{0:T(256)} %param.27) | copy-start | bytes 3076
  9.5 344.0 %copy-start.6 = (f32[512]{0:T(512)S(1)}, f32[512]{0:T(512)}, u32[]{:S(2)}) copy-start(f32[512]{0:T(512)} %param.24) | copy-start | bytes 6148
  9.5 346.3 %copy-start.9 = (f32[192]{0:T(256)S(1)}, f32[192]{0:T(256)}, u32[]{:S(2)}) copy-start(f32[192]{0:T(256)} %param.28) | copy-start | bytes 2308
  9.5 348.7 %copy-start.7 = (f32[512]{0:T(512)S(1)}, f32[512]{0:T(512)}, u32[]{:S(2)}) copy-start(f32[512]{0:T(512)} %param.26) | copy-start | bytes 6148
  336.3 93.7 %copy-start.4 = (f32[96]{0:T(128)}, f32[96]{0:T(128)S(1)}, u32[]{:S(2)}) copy-start(f32[96]{0:T(128)S(1)} %get-tuple-element.73) | copy-start | bytes 1156
  337.6 92.4 %copy-start.5 = (f32[96]{0:T(128)}, f32[96]{0:T(128)S(1)}, u32[]{:S(2)}) copy-start(f32[96]{0:T(128)S(1)} %get-tuple-element.75) | copy-start | bytes 1156
  338.8 91.2 %copy-start.2 = (f32[256]{0:T(256)}, f32[256]{0:T(256)S(1)}, u32[]{:S(2)}) copy-start(f32[256]{0:T(256)S(1)} %get-tuple-element.77) | copy-start | bytes 3076
  354.2 75.8 %copy-start = (f32[512]{0:T(512)}, f32[512]{0:T(512)S(1)}, u32[]{:S(2)}) copy-start(f32[512]{0:T(512)S(1)} %multiply_add_fusion.3) | copy-start | bytes 6148
  356.5 73.5 %copy-start.3 = (f32[192]{0:T(256)}, f32[192]{0:T(256)S(1)}, u32[]{:S(2)}) copy-start(f32[192]{0:T(256)S(1)} %multiply_add_fusion.4) | copy-start | bytes 2308
  358.8 71.2 %copy-start.1 = (f32[512]{0:T(512)}, f32[512]{0:T(512)S(1)}, u32[]{:S(2)}) copy-start(f32[512]{0:T(512)S(1)} %multiply_add_fusion.2) | copy-start | bytes 6148

commit v2 on v1

--- a/solution.py
+++ b/solution.py
@@ -1,5 +1,3 @@
-import functools
-
 import jax
 import jax.numpy as jnp
 from jax import lax
@@ -9,7 +7,7 @@
 
 EPS_ONE = 1e-30
 EPS_TWO = 1e-3
-CHUNKS = 16
+CHUNKS = 32
 NZ = 4
 NR = 8
 HOME_LAG = (3, 2, 2, 3)
@@ -30,12 +28,13 @@
 
 
 def kernel(
-    xt, xa, dyg, dyu, dydt, wg, wu, wdt,
-    outt, oact, gg, gu, gdt,
+    xt, xa, dyg, dyu, dydt, wgf, wuf, wdf, rg, cg, ru, cu, rd, cd, hp,
+    outt, oact, gg, gu, gdt, sv,
     rsu, rsd, ag, dz, dxy, wall, part, txt, txa, tg, tu, td, dloc, st,
+    wg, wu, wdt, sa, sb, s1, s2,
     tile_sem, dloc_sem, rsu_r, rsd_r, ag_r, dz_r, dxy_r, w_r, wp_r,
-    rsu_s, rsd_s, agu_s, agd_s, dzu_s, dzd_s, dxy_s, w_s, wp_s, wl_s,
-    out_sem, st_l, st_s, oact_r,
+    rsu_s, rsd_s, agu_s, agd_s, dzu_s, dzd_s, dxy_s, wu_s, wd_s, wp_s,
+    out_sem, st_l, st_s, oact_r, small_s, small_r,
 ):
     z = lax.axis_index("col")
     i = lax.axis_index("row")
@@ -63,20 +62,14 @@
         )
 
     barrier = pltpu.get_barrier_semaphore()
-    peers = [base + q for q in plane_peers] + [base + partner]
-    peers += [((z + d) % NZ) * NR + i for d in (1, 2, 3)]
-    for dev in peers:
-        pl.semaphore_signal(barrier, inc=1, device_id=dev, device_id_type=pl.DeviceIdType.LOGICAL)
-
-    def order(j):
-        odd = j % 2
-        return (1 - odd) * (3 - j // 2) + odd * (j // 2)
-
-    def tile_at(k, j):
-        h = order(j)
-        lag = jnp.where(h > z, z, jnp.where(h < z, NZ - 1 - z, jnp.maximum(z, NZ - 1 - z)))
-        c = k - lag
-        return h, c, jnp.logical_and(c >= 0, c < C)
+    me = base + i
+    ndev = NZ * NR
+
+    def greet(d, carry):
+        pl.semaphore_signal(barrier, inc=1, device_id=(me + d) % ndev, device_id_type=pl.DeviceIdType.LOGICAL)
+        return carry
+
+    lax.fori_loop(1, ndev, greet, 0)
 
     def tile_copies(h, c, slot):
         t0 = pl.multiple_of(h * home_len + c * S, S)
@@ -89,10 +82,8 @@
             pltpu.make_async_copy(dydt.at[:, rows], td.at[slot], tile_sem.at[slot, 4]),
         ]
 
-    def start_tile(k, j, slot):
-        h, c, on = tile_at(k, j)
-
-        @pl.when(on)
+    def start_tile(h, c, slot):
+        @pl.when(c < C)
         def _():
             for cp in tile_copies(h, c, slot):
                 cp.start()
@@ -127,21 +118,155 @@
         return pltpu.make_async_copy(
             ag.at[h, c], outt.at[:, pl.ds(pl.multiple_of(h * home_len + c * S, S), S)], out_sem.at[0])
 
-    def w_copy(d):
-        return rcopy(wdt, wall.at[0, NZ - d], w_s.at[d - 1], w_r.at[NZ - d - 1], ((z + d) % NZ) * NR + i)
-
     wp_copy = rcopy(wall.at[0], wall.at[1], wp_s.at[0], wp_r.at[0], base + partner)
 
-    start_tile(0, 0, 0)
+    def scalar_copy(ref, t, d):
+        return rcopy(ref.at[me], ref.at[me], small_s.at[t], small_r.at[t], (me + d) % ndev)
+
+    def row_copy(d):
+        return rcopy(sa.at[i], sa.at[i], small_s.at[0], small_r.at[0], base + (i + d) % NR)
+
+    def col_copy(d):
+        return rcopy(sb.at[z], sb.at[z], small_s.at[1], small_r.at[1], ((z + d) % NZ) * NR + i)
+
+    def lanes_of(v, width):
+        n = v.shape[0]
+        r_id = lax.broadcasted_iota(jnp.int32, (n, width), 0)
+        l_id = lax.broadcasted_iota(jnp.int32, (n, width), 1)
+        return jnp.sum(jnp.where(r_id == l_id, v, 0.0), axis=0, keepdims=True)
+
+    def column_of(v, n):
+        width = v.shape[1]
+        r_id = lax.broadcasted_iota(jnp.int32, (n, width), 0)
+        l_id = lax.broadcasted_iota(jnp.int32, (n, width), 1)
+        return jnp.sum(jnp.where(r_id == l_id, v, 0.0), axis=1, keepdims=True)
+
+    def total(v):
+        return jnp.sum(jnp.sum(v, axis=1, keepdims=True), axis=0, keepdims=True)
+
+    def pack_lanes(vals):
+        lane = lax.broadcasted_iota(jnp.int32, (1, 128), 1)
+        out = jnp.zeros((1, 128), F32)
+        for t, v in enumerate(vals):
+            out = jnp.where(lane == t, v, out)
+        return out
+
+    def lane_value(v, t):
+        lane = lax.broadcasted_iota(jnp.int32, (1, 128), 1)
+        return jnp.sum(jnp.where(lane == t, v, 0.0), axis=1, keepdims=True)
+
+    m_gu = NR * gg.shape[0]
+    n_gu = NZ * gg.shape[1]
+    m_dn = NR * gdt.shape[1]
+    n_dn = NZ * gdt.shape[0]
+    mg = gg.shape[0]
+    ng = gg.shape[1]
+    md = gdt.shape[1]
+    nd = gdt.shape[0]
+    beta = hp[0]
+    rho = hp[1]
+    dcut = hp[2]
+
+    def first_sums():
+        tot = []
+        for t, ref in enumerate((gg, gu)):
+            g = ref[...]
+            q = g * g + EPS_ONE
+            rows = jnp.sum(q, axis=1, keepdims=True)
+            sa[i, t] = jnp.sum(q, axis=0, keepdims=True)
+            sb[z, t, :, pl.ds(0, 128)] = lanes_of(rows, 128)
+            tot.append(total(rows))
+        g = gdt[...]
+        q = g * g + EPS_ONE
+        n_sum = jnp.sum(q, axis=1, keepdims=True)
+        sa[i, 2, :, pl.ds(0, 256)] = lanes_of(n_sum, 256)
+        sb[z, 2] = jnp.sum(q, axis=0, keepdims=True)
+        tot.append(total(n_sum))
+        for ref in (wgf, wuf, wdf):
+            w = ref[...]
+            tot.append(total(w * w))
+        for ref in (rg, ru, rd):
+            tot.append(total(ref[...]))
+        s1[me] = pack_lanes(tot)
+        for d in range(1, NR):
+            row_copy(d).start()
+        for d in range(1, NZ):
+            col_copy(d).start()
+
+        def send(d, carry):
+            scalar_copy(s1, 2, d).start()
+            return carry
+
+        lax.fori_loop(1, ndev, send, 0)
+
+    def second_sums():
+        some = sa.at[pl.ds(0, NR - 1)]
+        rcopy(some, some, small_s.at[0], small_r.at[0], base + partner).wait_recv()
+        some = sb.at[pl.ds(0, NZ - 1)]
+        rcopy(some, some, small_s.at[1], small_r.at[1], base + partner).wait_recv()
+        some = s1.at[pl.ds(0, ndev - 1)]
+        rcopy(some, some, small_s.at[2], small_r.at[2], base + partner).wait_recv()
+        tot = jnp.sum(s1[...], axis=0)
+        asum = jnp.sum(sa[...], axis=0)
+        bsum = jnp.sum(sb[...], axis=0)
+        u_sq = []
+        for t, (gref, rref, cref) in enumerate(((gg, rg, cg), (gu, ru, cu))):
+            r_new = beta * rref[...] + (1.0 - beta) * (bsum[t][:, :mg] / n_gu)
+            c_new = beta * cref[...] + (1.0 - beta) * (asum[t] / m_gu)
+            q_mean = lane_value(tot, t) / (m_gu * n_gu)
+            r_mean = beta * (lane_value(tot, 6 + t) / (NZ * m_gu)) + (1.0 - beta) * q_mean
+            sv[pl.ds(2 * t, 1), pl.ds(0, mg)] = r_new
+            sv[pl.ds(2 * t + 1, 1), :] = c_new
+            u = gref[...] * lax.rsqrt(column_of(r_new, mg) * c_new / r_mean)
+            gref[...] = u
+            u_sq.append(total(u * u))
+        r_new = beta * rd[...] + (1.0 - beta) * (bsum[2] / n_dn)
+        c_new = beta * cd[...] + (1.0 - beta) * (asum[2][:, :nd] / m_dn)
+        q_mean = lane_value(tot, 2) / (m_dn * n_dn)
+        r_mean = beta * (lane_value(tot, 8) / (NZ * m_dn)) + (1.0 - beta) * q_mean
+        sv[pl.ds(4, 1), pl.ds(0, md)] = r_new
+        sv[pl.ds(5, 1), pl.ds(0, nd)] = c_new
+        u = gdt[...] * lax.rsqrt(r_new * column_of(c_new, nd) / r_mean)
+        gdt[...] = u
+        u_sq.append(total(u * u))
+        s2[me] = pack_lanes(u_sq)
+
+        def send(d, carry):
+            scalar_copy(s2, 3, d).start()
+            return carry
+
+        lax.fori_loop(1, ndev, send, 0)
+        size = m_gu * n_gu
+        sv[pl.ds(6, 1), pl.ds(0, 128)] = pack_lanes(
+            [rho * jnp.maximum(EPS_TWO, jnp.sqrt(lane_value(tot, 3 + t) / size)) for t in range(3)])
+
+    def third_sums():
+        some = s2.at[pl.ds(0, ndev - 1)]
+        rcopy(some, some, small_s.at[3], small_r.at[3], base + partner).wait_recv()
+        rms_u = jnp.sqrt(jnp.sum(s2[...], axis=0) / (m_gu * n_gu))
+        sv[pl.ds(7, 1), pl.ds(0, 128)] = sv[pl.ds(6, 1), pl.ds(0, 128)] / jnp.maximum(1.0, rms_u / dcut)
+
+    for t, h in ((0, 3), (1, 0)):
+        start_tile(h, 0, t)
     gg[...] = jnp.zeros_like(gg)
     gu[...] = jnp.zeros_like(gu)
     gdt[...] = jnp.zeros_like(gdt)
-    wl = pltpu.make_async_copy(wdt, wall.at[0, 0], wl_s.at[0])
-    wl.start()
-    wl.wait()
-    pl.semaphore_wait(barrier, len(peers))
-    for d in (1, 2, 3):
-        w_copy(d).start()
+    sa[...] = jnp.zeros_like(sa)
+    sb[...] = jnp.zeros_like(sb)
+    sv[...] = jnp.zeros_like(sv)
+    wg[...] = wgf[...].astype(BF16)
+    wu[...] = wuf[...].astype(BF16)
+    wdt[...] = wdf[...].astype(BF16)
+    wall[0, 0] = wdt[...]
+    pl.semaphore_wait(barrier, ndev - 1)
+
+    @pl.when(z < NZ - 1)
+    def _():
+        rcopy(wdt, wall.at[0, 3], wu_s.at[0], w_r.at[2], up_id).start()
+
+    @pl.when(z > 0)
+    def _():
+        rcopy(wdt, wall.at[0, 1], wd_s.at[0], w_r.at[0], dn_id).start()
 
     def step(k, carry):
         @pl.when(k < C)
@@ -160,6 +285,22 @@
             c = k - d
             ok = jnp.logical_and(c >= 0, c < C)
 
+            @pl.when(jnp.logical_and(k == d, z >= d))
+            def _():
+                rcopy(wdt, wall.at[0, 4 - d], wu_s.at[0], w_r.at[3 - d], up_id).wait_recv()
+                if d < 3:
+                    @pl.when(z < NZ - 1)
+                    def _():
+                        rcopy(wall.at[0, 4 - d], wall.at[0, 3 - d], wu_s.at[d], w_r.at[2 - d], up_id).start()
+
+            @pl.when(jnp.logical_and(k == d, NZ - 1 - z >= d))
+            def _():
+                rcopy(wdt, wall.at[0, d], wd_s.at[0], w_r.at[d - 1], dn_id).wait_recv()
+                if d < 3:
+                    @pl.when(z > 0)
+                    def _():
+                        rcopy(wall.at[0, d], wall.at[0, d + 1], wd_s.at[d], w_r.at[d], dn_id).start()
+
             @pl.when(jnp.logical_and(ok, z >= d))
             def _():
                 rcopy(dz.at[c, 3 - d], dz.at[c, 3 - d], dzu_s.at[0], dz_r.at[3 - d, c], up_id).wait_recv()
@@ -203,86 +344,90 @@
 
                 out_copy(h, c).start()
 
-        def tile(j, carry2):
-            slot = j % 2
-            nj = j + 1
-            start_tile(k + nj // 4, nj % 4, nj % 2)
-            h, c, on = tile_at(k, j)
-
-            @pl.when(on)
-            def _():
-                for cp in tile_copies(h, c, slot):
+        @pl.when(k == C)
+        def _():
+            first_sums()
+
+        @pl.when(k == C + 2)
+        def _():
+            second_sums()
+
+        @pl.when(k == C + 4)
+        def _():
+            third_sums()
+
+        order = (3, 0, 2, 1)
+        for t, h in enumerate(order):
+            slot = t % 2
+
+            @pl.when(k < C)
+            def _():
+                for cp in tile_copies(h, k, slot):
                     cp.wait()
                 g = tg[slot]
                 u = tu[slot]
-                part[...] = mm_nt(wg[...], g) + mm_nt(wu[...], u)
-
-                @pl.when(h > z)
-                def _():
-                    @pl.when(z > 0)
-                    def _():
-                        rcopy(rsu.at[h - 1, c], rsu.at[h - 1, c], rsu_s.at[h - 1], rsu_r.at[h - 1, c], up_id).wait_recv()
-                        rsu[h - 1, c] = rsu[h - 1, c] + part[...]
-
-                    @pl.when(z == 0)
-                    def _():
-                        rsu[h - 1, c] = part[...]
-
-                    rcopy(rsu.at[h - 1, c], rsu.at[h - 1, c], rsu_s.at[h - 1], rsu_r.at[h - 1, c], up_id).start()
-
-                @pl.when(h < z)
-                def _():
-                    @pl.when(z < NZ - 1)
-                    def _():
-                        rcopy(rsd.at[h, c], rsd.at[h, c], rsd_s.at[h], rsd_r.at[h, c], dn_id).wait_recv()
-                        rsd[h, c] = rsd[h, c] + part[...]
-
-                    @pl.when(z == NZ - 1)
-                    def _():
-                        rsd[h, c] = part[...]
-
-                    rcopy(rsd.at[h, c], rsd.at[h, c], rsd_s.at[h], rsd_r.at[h, c], dn_id).start()
-
-                @pl.when(h == z)
-                def _():
-                    @pl.when(z > 0)
-                    def _():
-                        rcopy(rsu.at[h - 1, c], rsu.at[h - 1, c], rsu_s.at[h - 1], rsu_r.at[h - 1, c], up_id).wait_recv()
-                        part[...] = part[...] + rsu[h - 1, c]
-
-                    @pl.when(z < NZ - 1)
-                    def _():
-                        rcopy(rsd.at[h, c], rsd.at[h, c], rsd_s.at[h], rsd_r.at[h, c], dn_id).wait_recv()
-                        part[...] = part[...] + rsd[h, c]
-
-                    ag[h, c] = part[...].astype(BF16)
-
-                    @pl.when(z < NZ - 1)
-                    def _():
-                        rcopy(ag.at[h, c], ag.at[h, c], agu_s.at[h], ag_r.at[h, c], up_id).start()
-
-                    @pl.when(z > 0)
-                    def _():
-                        rcopy(ag.at[h, c], ag.at[h, c], agd_s.at[h], ag_r.at[h, c], dn_id).start()
-
-                    out_copy(h, c).start()
-
+                part[k % 4, h] = mm_nt(wg[...], g) + mm_nt(wu[...], u)
                 gg[...] += mm(txt[slot], g)
                 gu[...] += mm(txt[slot], u)
                 gdt[...] += mm(td[slot], txa[slot])
 
-            return carry2
-
-        lax.fori_loop(0, 4, tile, 0)
-
-        @pl.when(k == 1)
-        def _():
-            for d in (1, 2, 3):
-                w_copy(NZ - d).wait_send()
-                rcopy(wdt, wall.at[0, d], w_s.at[d - 1], w_r.at[d - 1], up_id).wait_recv()
+            start_tile(order[(t + 2) % 4], k + (t + 2) // 4, slot)
+
+            if h > 0:
+                c = k - z
+
+                @pl.when(jnp.logical_and(h > z, jnp.logical_and(c >= 0, c < C)))
+                def _():
+                    @pl.when(z > 0)
+                    def _():
+                        rcopy(rsu.at[h - 1, c], rsu.at[h - 1, c], rsu_s.at[h - 1], rsu_r.at[h - 1, c], up_id).wait_recv()
+                        rsu[h - 1, c] = rsu[h - 1, c] + part[c % 4, h]
+
+                    @pl.when(z == 0)
+                    def _():
+                        rsu[h - 1, c] = part[c % 4, h]
+
+                    rcopy(rsu.at[h - 1, c], rsu.at[h - 1, c], rsu_s.at[h - 1], rsu_r.at[h - 1, c], up_id).start()
+
+            if h < NZ - 1:
+                c2 = k - (NZ - 1 - z)
+
+                @pl.when(jnp.logical_and(h < z, jnp.logical_and(c2 >= 0, c2 < C)))
+                def _():
+                    @pl.when(z < NZ - 1)
+                    def _():
+                        rcopy(rsd.at[h, c2], rsd.at[h, c2], rsd_s.at[h], rsd_r.at[h, c2], dn_id).wait_recv()
+                        rsd[h, c2] = rsd[h, c2] + part[c2 % 4, h]
+
+                    @pl.when(z == NZ - 1)
+                    def _():
+                        rsd[h, c2] = part[c2 % 4, h]
+
+                    rcopy(rsd.at[h, c2], rsd.at[h, c2], rsd_s.at[h], rsd_r.at[h, c2], dn_id).start()
+
+            c3 = k - HOME_LAG[h]
+
+            @pl.when(jnp.logical_and(h == z, jnp.logical_and(c3 >= 0, c3 < C)))
+            def _():
+                acc = part[c3 % 4, h]
+                if h > 0:
+                    rcopy(rsu.at[h - 1, c3], rsu.at[h - 1, c3], rsu_s.at[h - 1], rsu_r.at[h - 1, c3], up_id).wait_recv()
+                    acc = acc + rsu[h - 1, c3]
+                if h < NZ - 1:
+                    rcopy(rsd.at[h, c3], rsd.at[h, c3], rsd_s.at[h], rsd_r.at[h, c3], dn_id).wait_recv()
+                    acc = acc + rsd[h, c3]
+                ag[h, c3] = acc.astype(BF16)
+                if h < NZ - 1:
+                    rcopy(ag.at[h, c3], ag.at[h, c3], agu_s.at[h], ag_r.at[h, c3], up_id).start()
+                if h > 0:
+                    rcopy(ag.at[h, c3], ag.at[h, c3], agd_s.at[h], ag_r.at[h, c3], dn_id).start()
+                out_copy(h, c3).start()
+
+        @pl.when(k == 3)
+        def _():
             wp_copy.start()
 
-        @pl.when(k == 3)
+        @pl.when(k == 5)
         def _():
             wp_copy.wait()
 
@@ -351,6 +496,17 @@
             @pl.when(jnp.logical_and(z <= h, z > 0))
             def _():
                 rcopy(ag.at[h], ag.at[h], agd_s.at[h], ag_r.at[h, 0], dn_id).wait_send()
+    for d in range(3):
+        @pl.when(jnp.logical_and(z >= d, z < NZ - 1))
+        def _():
+            rcopy(wdt, wdt, wu_s.at[d], w_r.at[0], up_id).wait_send()
+
+        @pl.when(jnp.logical_and(NZ - 1 - z >= d, z > 0))
+        def _():
+            rcopy(wdt, wdt, wd_s.at[d], w_r.at[0], dn_id).wait_send()
+    for t, (ref, cnt) in enumerate(((sa, NR - 1), (sb, NZ - 1), (s1, ndev - 1), (s2, ndev - 1))):
+        some = ref.at[pl.ds(0, cnt)]
+        rcopy(some, some, small_s.at[t], small_r.at[t], base + partner).wait_send()
     dzall = dxy.at[0, :, 0]
     for d in range(3):
         @pl.when(jnp.logical_and(z >= d, z < NZ - 1))
@@ -364,7 +520,7 @@
         rcopy(dz, dxy.at[s], dxy_s.at[s], dxy_r.at[s, 0], base + xn).wait_send()
 
 
-def main_call(xt, xa, dyg, dyu, dydt, wg, wu, wdt):
+def main_call(xt, xa, dyg, dyu, dydt, wg, wu, wdt, vecs, hp):
     T, ka = xa.shape
     m = xt.shape[0]
     n = dyg.shape[1]
@@ -375,6 +531,7 @@
     dma = pltpu.SemaphoreType.DMA
     anyspec = pl.BlockSpec(memory_space=pl.ANY)
     vspec = pl.BlockSpec(memory_space=pltpu.VMEM)
+    sspec = pl.BlockSpec(memory_space=pltpu.SMEM)
     scratch = [
         pltpu.VMEM((3, C, m, S), F32),
         pltpu.VMEM((3, C, m, S), F32),
@@ -382,7 +539,7 @@
         pltpu.VMEM((C, 3, nd, Sd), BF16),
         pltpu.VMEM((3, C, 3, nd, Sd), BF16),
         pltpu.VMEM((2, NZ, nd, ka), BF16),
-        pltpu.VMEM((m, S), F32),
+        pltpu.VMEM((4, NZ, m, S), F32),
         pltpu.VMEM((2, m, S), BF16),
         pltpu.VMEM((2, S, ka), BF16),
         pltpu.VMEM((2, S, n), BF16),
@@ -390,10 +547,17 @@
         pltpu.VMEM((2, nd, S), BF16),
         pltpu.VMEM((2, 4, nd, Sd), BF16),
         pltpu.VMEM((2, 2, 4, Sd, ka), BF16),
+        pltpu.VMEM((m, n), BF16),
+        pltpu.VMEM((m, n), BF16),
+        pltpu.VMEM((nd, ka), BF16),
+        pltpu.VMEM((NR, 3, 1, n), F32),
+        pltpu.VMEM((NZ, 3, 1, 256), F32),
+        pltpu.VMEM((NZ * NR, 1, 128), F32),
+        pltpu.VMEM((NZ * NR, 1, 128), F32),
         dma((2, 5)), dma((2, 4)),
         dma((3, C)), dma((3, C)), dma((NZ, C)), dma((3, C)), dma((3, C)), dma((3,)), dma((1,)),
-        dma((3,)), dma((3,)), dma((NZ,)), dma((NZ,)), dma((3,)), dma((3,)), dma((3,)), dma((3,)), dma((1,)), dma((1,)),
-        dma((1,)), dma((2, 4)), dma((2, 4)), dma((1,)),
+        dma((3,)), dma((3,)), dma((NZ,)), dma((NZ,)), dma((3,)), dma((3,)), dma((3,)), dma((3,)), dma((3,)), dma((1,)),
+        dma((1,)), dma((2, 4)), dma((2, 4)), dma((1,)), dma((4,)), dma((4,)),
     ]
     return pl.pallas_call(
         kernel,
@@ -403,35 +567,70 @@
             jax.ShapeDtypeStruct((m, n), F32),
             jax.ShapeDtypeStruct((m, n), F32),
             jax.ShapeDtypeStruct((nd, ka), F32),
+            jax.ShapeDtypeStruct((8, n), F32),
         ),
-        in_specs=[anyspec] * 5 + [vspec] * 3,
-        out_specs=(anyspec, anyspec, vspec, vspec, vspec),
+        in_specs=[anyspec] * 5 + [vspec] * 9 + [sspec],
+        out_specs=(anyspec, anyspec, vspec, vspec, vspec, vspec),
         scratch_shapes=scratch,
         compiler_params=pltpu.CompilerParams(
             collective_id=0, has_side_effects=True, vmem_limit_bytes=67_000_000),
-    )(xt, xa, dyg, dyu, dydt, wg, wu, wdt)
-
-
-def factored_step(w_loc, grad_loc, r_loc, c_loc, hyper_params, m_total, n_total):
-    beta_two = hyper_params[0]
-    grad_sq = grad_loc * grad_loc + EPS_ONE
-    row_sum = lax.psum(jnp.sum(grad_sq, axis=1), 'col')
-    col_sum = lax.psum(jnp.sum(grad_sq, axis=0), 'row')
-    r_new = beta_two * r_loc + (1.0 - beta_two) * (row_sum / n_total)
-    c_new = beta_two * c_loc + (1.0 - beta_two) * (col_sum / m_total)
-    r_mean = lax.psum(jnp.sum(r_new), 'row') / m_total
-    update = grad_loc * lax.rsqrt(r_new[:, None] * c_new[None, :] / r_mean)
-    u_sq = lax.psum(jnp.sum(update * update), ('row', 'col'))
-    rms_u = jnp.sqrt(u_sq / (m_total * n_total))
-    update_hat = update / jnp.maximum(1.0, rms_u / hyper_params[2])
-    w_sq = lax.psum(jnp.sum(w_loc * w_loc), ('row', 'col'))
-    step_size = hyper_params[1] * jnp.maximum(EPS_TWO, jnp.sqrt(w_sq / (m_total * n_total)))
-    return w_loc - step_size * update_hat, r_new, c_new
+    )(xt, xa, dyg, dyu, dydt, wg, wu, wdt, *vecs, hp)
+
+
+def final_kernel(
+    outt, oact, ug, uu, ud, sv, wg, wu, wd,
+    outt_o, oact_o, wg_o, wu_o, wd_o, rg_o, cg_o, ru_o, cu_o, rd_o, cd_o,
+    buft, bufa, in_t, in_a, out_t, out_a,
+):
+    nt = buft.shape[0]
+    na = bufa.shape[0]
+    ht = buft.shape[1]
+    ha = bufa.shape[1]
+    a_in = [pltpu.make_async_copy(oact.at[pl.ds(j * ha, ha), :], bufa.at[j], in_a.at[j]) for j in range(na)]
+    a_out = [pltpu.make_async_copy(bufa.at[j], oact_o.at[pl.ds(j * ha, ha), :], out_a.at[j]) for j in range(na)]
+    t_in = [pltpu.make_async_copy(outt.at[pl.ds(j * ht, ht), :], buft.at[j], in_t.at[j]) for j in range(nt)]
+    t_out = [pltpu.make_async_copy(buft.at[j], outt_o.at[pl.ds(j * ht, ht), :], out_t.at[j]) for j in range(nt)]
+    for cp in a_in + t_in:
+        cp.start()
+    for t, (u, w, o) in enumerate(((ug, wg, wg_o), (uu, wu, wu_o), (ud, wd, wd_o))):
+        o[...] = w[...] - sv[7:8, t:t + 1] * u[...]
+    for t, o in enumerate((rg_o, cg_o, ru_o, cu_o, rd_o, cd_o)):
+        o[...] = sv[t:t + 1, :o.shape[1]]
+    for cin, cout in zip(a_in + t_in, a_out + t_out):
+        cin.wait()
+        cout.start()
+    for cp in a_out + t_out:
+        cp.wait()
+
+
+def final_call(outt, oact, ug, uu, ud, sv, wg, wu, wd):
+    m, T = outt.shape
+    ka = oact.shape[1]
+    n = ug.shape[1]
+    nd = ud.shape[0]
+    nt = m // 16
+    na = 16
+    dma = pltpu.SemaphoreType.DMA
+    anyspec = pl.BlockSpec(memory_space=pl.ANY)
+    vspec = pl.BlockSpec(memory_space=pltpu.VMEM)
+    shape = jax.ShapeDtypeStruct
+    return pl.pallas_call(
+        final_kernel,
+        out_shape=(
+            shape((m, T), BF16), shape((T, ka), BF16),
+            shape((m, n), F32), shape((m, n), F32), shape((nd, ka), F32),
+            shape((1, m), F32), shape((1, n), F32), shape((1, m), F32), shape((1, n), F32),
+            shape((1, ka), F32), shape((1, nd), F32)),
+        in_specs=[anyspec] * 2 + [vspec] * 7,
+        out_specs=(anyspec,) * 2 + (vspec,) * 9,
+        scratch_shapes=[
+            pltpu.VMEM((nt, m // nt, T), BF16), pltpu.VMEM((na, T // na, ka), BF16),
+            dma((nt,)), dma((na,)), dma((nt,)), dma((na,))],
+        compiler_params=pltpu.CompilerParams(vmem_limit_bytes=64_000_000),
+    )(outt, oact, ug, uu, ud, sv, wg, wu, wd)
 
 
 def solution(mesh):
-    row_size = mesh.shape['row']
-    col_size = mesh.shape['col']
     weight_spec = P('row', 'col')
     act_spec = P(None, 'row')
     grad_spec = P(None, 'col')
@@ -439,14 +638,12 @@
     out_specs = (weight_spec,) * 3 + (P('row'), P('col')) * 3 + (act_spec, act_spec)
 
     def body(w_gate, w_up, w_down, x_norm, x_act, dy_gate, dy_up, dy_down, r_gate, c_gate, r_up, c_up, r_down, c_down, hyper_params):
-        d_model = w_gate.shape[0] * row_size
-        d_ff = w_gate.shape[1] * col_size
-        outt, dx_act, g_gate, g_up, g_down_t = main_call(
-            x_norm.T, x_act, dy_gate, dy_up, dy_down.T,
-            w_gate.astype(BF16), w_up.astype(BF16), w_down.T.astype(BF16))
-        new_gate, r_gate_new, c_gate_new = factored_step(w_gate, g_gate, r_gate, c_gate, hyper_params, d_model, d_ff)
-        new_up, r_up_new, c_up_new = factored_step(w_up, g_up, r_up, c_up, hyper_params, d_model, d_ff)
-        new_down, r_down_new, c_down_new = factored_step(w_down, g_down_t.T, r_down, c_down, hyper_params, d_ff, d_model)
-        return (new_gate, new_up, new_down, r_gate_new, c_gate_new, r_up_new, c_up_new, r_down_new, c_down_new, outt.T, dx_act)
+        wdt = w_down.T
+        vecs = [v.reshape(1, -1) for v in (r_gate, c_gate, r_up, c_up, r_down, c_down)]
+        outt, oact, ug, uu, ud, sv = main_call(
+            x_norm.T, x_act, dy_gate, dy_up, dy_down.T, w_gate, w_up, wdt, vecs, hyper_params)
+        outt, dx_act, new_gate, new_up, new_down_t, *stats = final_call(outt, oact, ug, uu, ud, sv, w_gate, w_up, wdt)
+        stats = [v.reshape(-1) for v in stats]
+        return (new_gate, new_up, new_down_t.T, *stats, outt.T, dx_act)
 
     return jax.shard_map(body, mesh=mesh, in_specs=in_specs, out_specs=out_specs, check_vma=False)

time: 432 us -> 327 us (0.76)
  blocking collectives: 61.2 us -> 0 us
  other arithmetic: 24.7 us -> 0 us
  local copies, waits for them, and re-layouts: 21.1 us -> 0 us
  Pallas kernels: 312 us -> 325 us
  between operations: 11.2 us -> 0.66 us
    psum x3 -> x0, blocking collectives: 61.2 us -> none  [the longest x1 38 us: factored_step(): u_sq = lax.psum(jnp.sum(update * update), ('row', 'col'))]
    unnamed x26 -> x0, local copies, waits for them, and re-layouts: 19.7 us -> none
    reduce_sum x12 -> x0, other arithmetic: 18.8 us -> none  [the longest x3 6.85 us: factored_step(): w_sq = lax.psum(jnp.sum(w_loc * w_loc), ('row', 'col'))]
    pallas_call x0 -> x1, Pallas kernels: none -> 18.1 us  [final_call(): pl.pallas_call(final_kernel, out_shape=(shape((m, T), BF16), shape((T, ka...]
    pallas_call x1, Pallas kernels: 312 us -> 307 us  [main_call(): pl.pallas_call(kernel, out_shape=(jax.ShapeDtypeStruct((m, T), BF16), jax...]
where the time goes in v2:
time: 327 us; the launch traced here: 326 us
  Pallas kernels  325 us (99%)
    pallas_call x1, Pallas kernels, main_call(): pl.pallas_call(kernel, out_shape=(jax.ShapeDtypeStruct((m, T), BF16), jax...  307 us
    pallas_call x1, Pallas kernels, final_call(): pl.pallas_call(final_kernel, out_shape=(shape((m, T), BF16), shape((T, ka...  18.1 us

profile of v2, /device:TPU:0, one launch (start us, length us, event | category | flops | bytes accessed | tf_op | source)
XLA Modules:
  0.0 325.5 jit_solution(400198931279170506)
XLA Ops:
  0.6 306.8 %shard_map.230 = (bf16[96,32768]{1,0:T(8,128)(2,1)}, bf16[32768,256]{1,0:T(8,128)(2,1)}, f32[96,512]{1,0:T(8,128)}, f32[96,512]{1,0:T(8,128)}, f32[192,256]{1,0:T(8,128)}, /*index=5*/f32[8,512]{1,0:T(8,128)}) custom-call(bf16[96,32768]{1,0:T(8,128)(2,1)} %bitcast.18, bf16[32768,256]{1,0:T(8,128)(2,1)} %xa.1, bf16[32768,512]{1,0:T(8,128)(2,1)} %dyg.1, ...), custom_call_target="tpu_custom_call" | custom-call | tf_op jit(solution)/shard_map/pallas_call | solution.py:562
  307.4 18.1 %shard_map.231 = (bf16[96,32768]{1,0:T(8,128)(2,1)}, bf16[32768,256]{1,0:T(8,128)(2,1)}, f32[96,512]{1,0:T(8,128)}, f32[96,512]{1,0:T(8,128)}, f32[192,256]{1,0:...) custom-call(bf16[96,32768]{1,0:T(8,128)(2,1)} %get-tuple-element.28., ...), custom_call_target="tpu_custom_call" | custom-call | tf_op jit(solution)/shard_map/pallas_call | solution.py:617

commit v3 on v2

--- a/solution.py
+++ b/solution.py
@@ -11,6 +11,10 @@
 NZ = 4
 NR = 8
 HOME_LAG = (3, 2, 2, 3)
+SKEW = (0, 2, 2, 0)
+AHEAD = 3
+SLOTS = 8
+DRAIN = 6
 F32 = jnp.float32
 BF16 = jnp.bfloat16
 
@@ -29,12 +33,12 @@
 
 def kernel(
     xt, xa, dyg, dyu, dydt, wgf, wuf, wdf, rg, cg, ru, cu, rd, cd, hp,
-    outt, oact, gg, gu, gdt, sv,
-    rsu, rsd, ag, dz, dxy, wall, part, txt, txa, tg, tu, td, dloc, st,
+    ag, oact, gg, gu, gdt, sv,
+    rsu, rsd, dz, dxy, wall, part, txt, txa, tg, tu, td, dloc, st,
     wg, wu, wdt, sa, sb, s1, s2,
     tile_sem, dloc_sem, rsu_r, rsd_r, ag_r, dz_r, dxy_r, w_r, wp_r,
     rsu_s, rsd_s, agu_s, agd_s, dzu_s, dzd_s, dxy_s, wu_s, wd_s, wp_s,
-    out_sem, st_l, st_s, oact_r, small_s, small_r,
+    st_s, oact_r, small_s, small_r,
 ):
     z = lax.axis_index("col")
     i = lax.axis_index("row")
@@ -61,6 +65,24 @@
             src, dst, ssem, rsem, device_id=dev, device_id_type=pl.DeviceIdType.LOGICAL
         )
 
+    def up_sum(h, c):
+        return rcopy(rsu.at[h - 1, c], rsu.at[h - 1, c], rsu_s.at[h - 1], rsu_r.at[h - 1, c], up_id)
+
+    def dn_sum(h, c):
+        return rcopy(rsd.at[h, c], rsd.at[h, c], rsd_s.at[h], rsd_r.at[h, c], dn_id)
+
+    def up_block(h, c):
+        return rcopy(ag.at[h, c], ag.at[h, c], agu_s.at[h], ag_r.at[h, c], up_id)
+
+    def dn_block(h, c):
+        return rcopy(ag.at[h, c], ag.at[h, c], agd_s.at[h], ag_r.at[h, c], dn_id)
+
+    def both(a, b):
+        return jnp.logical_and(a, b)
+
+    def valid(c):
+        return both(c >= 0, c < C)
+
     barrier = pltpu.get_barrier_semaphore()
     me = base + i
     ndev = NZ * NR
@@ -83,7 +105,7 @@
         ]
 
     def start_tile(h, c, slot):
-        @pl.when(c < C)
+        @pl.when(valid(c))
         def _():
             for cp in tile_copies(h, c, slot):
                 cp.start()
@@ -96,27 +118,16 @@
             for s, q in enumerate((i,) + plane_peers)
         ]
 
-    def st_local(c, slot):
-        return [
-            pltpu.make_async_copy(
-                st.at[slot, 0, s],
-                oact.at[pl.ds(pl.multiple_of(q * eighth + c * Sd, Sd), Sd), :],
-                st_l.at[slot, s])
-            for s, q in enumerate((i,) + plane_peers)
-        ]
+    def act_rows(q, c):
+        return pl.ds(pl.multiple_of(q * eighth + c * Sd, Sd), Sd)
 
     def st_remote(c, slot):
         return [
             rcopy(
-                st.at[slot, 1, s],
-                oact.at[pl.ds(pl.multiple_of(q * eighth + c * Sd, Sd), Sd), :],
+                st.at[slot, s], oact.at[act_rows(q, c), :],
                 st_s.at[slot, s], oact_r.at[0], base + partner)
             for s, q in enumerate((i,) + plane_peers)
         ]
-
-    def out_copy(h, c):
-        return pltpu.make_async_copy(
-            ag.at[h, c], outt.at[:, pl.ds(pl.multiple_of(h * home_len + c * S, S), S)], out_sem.at[0])
 
     wp_copy = rcopy(wall.at[0], wall.at[1], wp_s.at[0], wp_r.at[0], base + partner)
 
@@ -268,24 +279,33 @@
     def _():
         rcopy(wdt, wall.at[0, 1], wd_s.at[0], w_r.at[0], dn_id).start()
 
+    def send_own(c):
+        @pl.when(c < C)
+        def _():
+            src = dydt.at[:, pl.ds(pl.multiple_of(i * eighth + c * Sd, Sd), Sd)]
+
+            @pl.when(z < NZ - 1)
+            def _():
+                rcopy(src, dz.at[c, 2], dzu_s.at[0], dz_r.at[2, c], up_id).start()
+
+            @pl.when(z > 0)
+            def _():
+                rcopy(src, dz.at[c, 0], dzd_s.at[0], dz_r.at[0, c], dn_id).start()
+
+    def run_ahead(c, carry):
+        send_own(c)
+        return carry
+
+    lax.fori_loop(0, AHEAD, run_ahead, 0)
+
     def step(k, carry):
-        @pl.when(k < C)
-        def _():
-            src = dydt.at[:, pl.ds(pl.multiple_of(i * eighth + k * Sd, Sd), Sd)]
-
-            @pl.when(z < NZ - 1)
-            def _():
-                rcopy(src, dz.at[k, 2], dzu_s.at[0], dz_r.at[2, k], up_id).start()
-
-            @pl.when(z > 0)
-            def _():
-                rcopy(src, dz.at[k, 0], dzd_s.at[0], dz_r.at[0, k], dn_id).start()
+        send_own(k + AHEAD)
 
         for d in (1, 2, 3):
             c = k - d
-            ok = jnp.logical_and(c >= 0, c < C)
-
-            @pl.when(jnp.logical_and(k == d, z >= d))
+            ok = valid(c)
+
+            @pl.when(both(k == d, z >= d))
             def _():
                 rcopy(wdt, wall.at[0, 4 - d], wu_s.at[0], w_r.at[3 - d], up_id).wait_recv()
                 if d < 3:
@@ -293,7 +313,7 @@
                     def _():
                         rcopy(wall.at[0, 4 - d], wall.at[0, 3 - d], wu_s.at[d], w_r.at[2 - d], up_id).start()
 
-            @pl.when(jnp.logical_and(k == d, NZ - 1 - z >= d))
+            @pl.when(both(k == d, NZ - 1 - z >= d))
             def _():
                 rcopy(wdt, wall.at[0, d], wd_s.at[0], w_r.at[d - 1], dn_id).wait_recv()
                 if d < 3:
@@ -301,7 +321,7 @@
                     def _():
                         rcopy(wall.at[0, d], wall.at[0, d + 1], wd_s.at[d], w_r.at[d], dn_id).start()
 
-            @pl.when(jnp.logical_and(ok, z >= d))
+            @pl.when(both(ok, z >= d))
             def _():
                 rcopy(dz.at[c, 3 - d], dz.at[c, 3 - d], dzu_s.at[0], dz_r.at[3 - d, c], up_id).wait_recv()
                 if d < 3:
@@ -309,7 +329,7 @@
                     def _():
                         rcopy(dz.at[c, 3 - d], dz.at[c, 2 - d], dzu_s.at[d], dz_r.at[2 - d, c], up_id).start()
 
-            @pl.when(jnp.logical_and(ok, NZ - 1 - z >= d))
+            @pl.when(both(ok, NZ - 1 - z >= d))
             def _():
                 rcopy(dz.at[c, d - 1], dz.at[c, d - 1], dzd_s.at[0], dz_r.at[d - 1, c], dn_id).wait_recv()
                 if d < 3:
@@ -319,109 +339,105 @@
 
         cx = k - 3
 
-        @pl.when(jnp.logical_and(cx >= 0, cx < C))
+        @pl.when(valid(cx))
         def _():
             for s, q in enumerate(plane_peers):
-                rcopy(dz.at[cx], dxy.at[s, cx], dxy_s.at[s], dxy_r.at[s, cx], base + q).start()
+                rcopy(dz.at[cx], dxy.at[s, cx % SLOTS], dxy_s.at[s], dxy_r.at[s, cx], base + q).start()
 
         for h in range(NZ):
             dist = jnp.abs(z - h)
-            c = k - HOME_LAG[h] - dist
-
-            @pl.when(jnp.logical_and(jnp.logical_and(c >= 0, c < C), z != h))
-            def _():
-                rcopy(ag.at[h, c], ag.at[h, c], agu_s.at[h], ag_r.at[h, c], up_id).wait_recv()
+            c = k - HOME_LAG[h] - SKEW[h] - dist
+
+            @pl.when(both(valid(c), z != h))
+            def _():
+                up_block(h, c).wait_recv()
 
                 if h < NZ - 2:
-                    @pl.when(jnp.logical_and(z > h, z < NZ - 1))
-                    def _():
-                        rcopy(ag.at[h, c], ag.at[h, c], agu_s.at[h], ag_r.at[h, c], up_id).start()
+                    @pl.when(both(z > h, z < NZ - 1))
+                    def _():
+                        up_block(h, c).start()
 
                 if h > 1:
-                    @pl.when(jnp.logical_and(z < h, z > 0))
-                    def _():
-                        rcopy(ag.at[h, c], ag.at[h, c], agd_s.at[h], ag_r.at[h, c], dn_id).start()
-
-                out_copy(h, c).start()
-
-        @pl.when(k == C)
+                    @pl.when(both(z < h, z > 0))
+                    def _():
+                        dn_block(h, c).start()
+
+
+        @pl.when(k == C + 2)
         def _():
             first_sums()
 
-        @pl.when(k == C + 2)
+        @pl.when(k == C + 4)
         def _():
             second_sums()
-
-        @pl.when(k == C + 4)
-        def _():
-            third_sums()
 
         order = (3, 0, 2, 1)
         for t, h in enumerate(order):
             slot = t % 2
-
-            @pl.when(k < C)
-            def _():
-                for cp in tile_copies(h, k, slot):
+            kt = k - SKEW[h]
+
+            @pl.when(valid(kt))
+            def _():
+                for cp in tile_copies(h, kt, slot):
                     cp.wait()
                 g = tg[slot]
                 u = tu[slot]
-                part[k % 4, h] = mm_nt(wg[...], g) + mm_nt(wu[...], u)
+                part[kt % 4, h] = mm_nt(wg[...], g) + mm_nt(wu[...], u)
                 gg[...] += mm(txt[slot], g)
                 gu[...] += mm(txt[slot], u)
                 gdt[...] += mm(td[slot], txa[slot])
 
-            start_tile(order[(t + 2) % 4], k + (t + 2) // 4, slot)
+            hn = order[(t + 2) % 4]
+            start_tile(hn, k + (t + 2) // 4 - SKEW[hn], slot)
 
             if h > 0:
-                c = k - z
-
-                @pl.when(jnp.logical_and(h > z, jnp.logical_and(c >= 0, c < C)))
+                c = kt - z
+
+                @pl.when(both(h > z, valid(c)))
                 def _():
                     @pl.when(z > 0)
                     def _():
-                        rcopy(rsu.at[h - 1, c], rsu.at[h - 1, c], rsu_s.at[h - 1], rsu_r.at[h - 1, c], up_id).wait_recv()
+                        up_sum(h, c).wait_recv()
                         rsu[h - 1, c] = rsu[h - 1, c] + part[c % 4, h]
 
                     @pl.when(z == 0)
                     def _():
                         rsu[h - 1, c] = part[c % 4, h]
 
-                    rcopy(rsu.at[h - 1, c], rsu.at[h - 1, c], rsu_s.at[h - 1], rsu_r.at[h - 1, c], up_id).start()
+                    up_sum(h, c).start()
 
             if h < NZ - 1:
-                c2 = k - (NZ - 1 - z)
-
-                @pl.when(jnp.logical_and(h < z, jnp.logical_and(c2 >= 0, c2 < C)))
+                c2 = kt - (NZ - 1 - z)
+
+                @pl.when(both(h < z, valid(c2)))
                 def _():
                     @pl.when(z < NZ - 1)
                     def _():
-                        rcopy(rsd.at[h, c2], rsd.at[h, c2], rsd_s.at[h], rsd_r.at[h, c2], dn_id).wait_recv()
+                        dn_sum(h, c2).wait_recv()
                         rsd[h, c2] = rsd[h, c2] + part[c2 % 4, h]
 
                     @pl.when(z == NZ - 1)
                     def _():
                         rsd[h, c2] = part[c2 % 4, h]
 
-                    rcopy(rsd.at[h, c2], rsd.at[h, c2], rsd_s.at[h], rsd_r.at[h, c2], dn_id).start()
-
-            c3 = k - HOME_LAG[h]
-
-            @pl.when(jnp.logical_and(h == z, jnp.logical_and(c3 >= 0, c3 < C)))
+                    dn_sum(h, c2).start()
+
+            c3 = kt - HOME_LAG[h]
+
+            @pl.when(both(h == z, valid(c3)))
             def _():
                 acc = part[c3 % 4, h]
                 if h > 0:
-                    rcopy(rsu.at[h - 1, c3], rsu.at[h - 1, c3], rsu_s.at[h - 1], rsu_r.at[h - 1, c3], up_id).wait_recv()
+                    up_sum(h, c3).wait_recv()
                     acc = acc + rsu[h - 1, c3]
                 if h < NZ - 1:
-                    rcopy(rsd.at[h, c3], rsd.at[h, c3], rsd_s.at[h], rsd_r.at[h, c3], dn_id).wait_recv()
+                    dn_sum(h, c3).wait_recv()
                     acc = acc + rsd[h, c3]
                 ag[h, c3] = acc.astype(BF16)
                 if h < NZ - 1:
-                    rcopy(ag.at[h, c3], ag.at[h, c3], agu_s.at[h], ag_r.at[h, c3], up_id).start()
+                    up_block(h, c3).start()
                 if h > 0:
-                    rcopy(ag.at[h, c3], ag.at[h, c3], agd_s.at[h], ag_r.at[h, c3], dn_id).start()
-                out_copy(h, c3).start()
+                    dn_block(h, c3).start()
 
         @pl.when(k == 3)
         def _():
@@ -433,7 +449,7 @@
 
         cf = k - 4
 
-        @pl.when(jnp.logical_and(cf >= 0, cf < C))
+        @pl.when(valid(cf))
         def _():
             for cp in dloc_copies(cf, cf % 2):
                 cp.start()
@@ -441,44 +457,39 @@
         ca = k - 5
         slot_a = ca % 2
 
-        @pl.when(jnp.logical_and(ca >= 0, ca < C))
+        @pl.when(valid(ca))
         def _():
             @pl.when(ca >= 2)
             def _():
-                for cp in st_local(ca - 2, slot_a):
-                    cp.wait()
                 for cp in st_remote(ca - 2, slot_a):
                     cp.wait_send()
 
             locs = dloc_copies(ca, slot_a)
-            outl = st_local(ca, slot_a)
             outr = st_remote(ca, slot_a)
-            for s in range(4):
+            for s, q in enumerate((i,) + plane_peers):
                 locs[s].wait()
                 if s == 0:
                     far = dz[ca]
                 else:
-                    rcopy(dz.at[ca], dxy.at[s - 1, ca], dxy_s.at[s - 1], dxy_r.at[s - 1, ca], base + xn).wait_recv()
-                    far = dxy[s - 1, ca]
+                    rcopy(dz.at[ca], dxy.at[s - 1, ca % SLOTS], dxy_s.at[s - 1], dxy_r.at[s - 1, ca], base + xn).wait_recv()
+                    far = dxy[s - 1, ca % SLOTS]
                 lhs = jnp.concatenate([dloc[slot_a, s], far.reshape(3 * far.shape[1], Sd)], axis=0)
-                for b in range(2):
-                    w = wall[b].reshape(lhs.shape[0], wall.shape[3])
-                    st[slot_a, b, s] = mm_tn(lhs, w).astype(BF16)
-                outl[s].start()
+                w = wall[1].reshape(lhs.shape[0], wall.shape[3])
+                st[slot_a, s] = mm_tn(lhs, w).astype(BF16)
                 outr[s].start()
+                w = wall[0].reshape(lhs.shape[0], wall.shape[3])
+                oact[act_rows(q, ca), :] = mm_tn(lhs, w).astype(BF16)
 
         return carry
 
-    lax.fori_loop(0, C + 6, step, 0)
+    lax.fori_loop(0, C + DRAIN, step, 0)
+    third_sums()
 
     for c in (C - 2, C - 1):
-        for cp in st_local(c, c % 2):
-            cp.wait()
         for cp in st_remote(c, c % 2):
             cp.wait_send()
     half = oact.at[pl.ds(0, T // 2), :]
     rcopy(half, half, st_s.at[0, 0], oact_r.at[0], base + partner).wait_recv()
-    pltpu.make_async_copy(outt, outt, out_sem.at[0]).wait()
     for h in (1, 2, 3):
         @pl.when(h > z)
         def _():
@@ -489,35 +500,35 @@
             rcopy(rsd.at[h], rsd.at[h], rsd_s.at[h], rsd_r.at[h, 0], dn_id).wait_send()
     for h in range(NZ):
         if h < NZ - 1:
-            @pl.when(jnp.logical_and(z >= h, z < NZ - 1))
+            @pl.when(both(z >= h, z < NZ - 1))
             def _():
                 rcopy(ag.at[h], ag.at[h], agu_s.at[h], ag_r.at[h, 0], up_id).wait_send()
         if h > 0:
-            @pl.when(jnp.logical_and(z <= h, z > 0))
+            @pl.when(both(z <= h, z > 0))
             def _():
                 rcopy(ag.at[h], ag.at[h], agd_s.at[h], ag_r.at[h, 0], dn_id).wait_send()
     for d in range(3):
-        @pl.when(jnp.logical_and(z >= d, z < NZ - 1))
+        @pl.when(both(z >= d, z < NZ - 1))
         def _():
             rcopy(wdt, wdt, wu_s.at[d], w_r.at[0], up_id).wait_send()
 
-        @pl.when(jnp.logical_and(NZ - 1 - z >= d, z > 0))
+        @pl.when(both(NZ - 1 - z >= d, z > 0))
         def _():
             rcopy(wdt, wdt, wd_s.at[d], w_r.at[0], dn_id).wait_send()
     for t, (ref, cnt) in enumerate(((sa, NR - 1), (sb, NZ - 1), (s1, ndev - 1), (s2, ndev - 1))):
         some = ref.at[pl.ds(0, cnt)]
         rcopy(some, some, small_s.at[t], small_r.at[t], base + partner).wait_send()
-    dzall = dxy.at[0, :, 0]
+    dzall = dz.at[:, 0]
     for d in range(3):
-        @pl.when(jnp.logical_and(z >= d, z < NZ - 1))
+        @pl.when(both(z >= d, z < NZ - 1))
         def _():
             rcopy(dzall, dzall, dzu_s.at[d], dz_r.at[0, 0], up_id).wait_send()
 
-        @pl.when(jnp.logical_and(NZ - 1 - z >= d, z > 0))
+        @pl.when(both(NZ - 1 - z >= d, z > 0))
         def _():
             rcopy(dzall, dzall, dzd_s.at[d], dz_r.at[0, 0], dn_id).wait_send()
     for s in range(3):
-        rcopy(dz, dxy.at[s], dxy_s.at[s], dxy_r.at[s, 0], base + xn).wait_send()
+        rcopy(dz, dz, dxy_s.at[s], dxy_r.at[s, 0], base + xn).wait_send()
 
 
 def main_call(xt, xa, dyg, dyu, dydt, wg, wu, wdt, vecs, hp):
@@ -535,9 +546,8 @@
     scratch = [
         pltpu.VMEM((3, C, m, S), F32),
         pltpu.VMEM((3, C, m, S), F32),
-        pltpu.VMEM((NZ, C, m, S), BF16),
         pltpu.VMEM((C, 3, nd, Sd), BF16),
-        pltpu.VMEM((3, C, 3, nd, Sd), BF16),
+        pltpu.VMEM((3, SLOTS, 3, nd, Sd), BF16),
         pltpu.VMEM((2, NZ, nd, ka), BF16),
         pltpu.VMEM((4, NZ, m, S), F32),
         pltpu.VMEM((2, m, S), BF16),
@@ -546,7 +556,7 @@
         pltpu.VMEM((2, S, n), BF16),
         pltpu.VMEM((2, nd, S), BF16),
         pltpu.VMEM((2, 4, nd, Sd), BF16),
-        pltpu.VMEM((2, 2, 4, Sd, ka), BF16),
+        pltpu.VMEM((2, 4, Sd, ka), BF16),
         pltpu.VMEM((m, n), BF16),
         pltpu.VMEM((m, n), BF16),
         pltpu.VMEM((nd, ka), BF16),
@@ -557,60 +567,54 @@
         dma((2, 5)), dma((2, 4)),
         dma((3, C)), dma((3, C)), dma((NZ, C)), dma((3, C)), dma((3, C)), dma((3,)), dma((1,)),
         dma((3,)), dma((3,)), dma((NZ,)), dma((NZ,)), dma((3,)), dma((3,)), dma((3,)), dma((3,)), dma((3,)), dma((1,)),
-        dma((1,)), dma((2, 4)), dma((2, 4)), dma((1,)), dma((4,)), dma((4,)),
+        dma((2, 4)), dma((1,)), dma((4,)), dma((4,)),
     ]
     return pl.pallas_call(
         kernel,
         out_shape=(
-            jax.ShapeDtypeStruct((m, T), BF16),
-            jax.ShapeDtypeStruct((T, ka), BF16),
-            jax.ShapeDtypeStruct((m, n), F32),
-            jax.ShapeDtypeStruct((m, n), F32),
-            jax.ShapeDtypeStruct((nd, ka), F32),
-            jax.ShapeDtypeStruct((8, n), F32),
+            pltpu.VMEM((NZ, C, m, S), BF16),
+            pltpu.VMEM((T, ka), BF16),
+            pltpu.VMEM((m, n), F32),
+            pltpu.VMEM((m, n), F32),
+            pltpu.VMEM((nd, ka), F32),
+            pltpu.VMEM((8, n), F32),
         ),
         in_specs=[anyspec] * 5 + [vspec] * 9 + [sspec],
-        out_specs=(anyspec, anyspec, vspec, vspec, vspec, vspec),
+        out_specs=(vspec,) * 6,
         scratch_shapes=scratch,
         compiler_params=pltpu.CompilerParams(
-            collective_id=0, has_side_effects=True, vmem_limit_bytes=67_000_000),
+            collective_id=0, has_side_effects=True, vmem_limit_bytes=40_000_000),
     )(xt, xa, dyg, dyu, dydt, wg, wu, wdt, *vecs, hp)
 
 
 def final_kernel(
-    outt, oact, ug, uu, ud, sv, wg, wu, wd,
+    ag, oact, ug, uu, ud, sv, wg, wu, wd,
     outt_o, oact_o, wg_o, wu_o, wd_o, rg_o, cg_o, ru_o, cu_o, rd_o, cd_o,
-    buft, bufa, in_t, in_a, out_t, out_a,
+    sem,
 ):
-    nt = buft.shape[0]
-    na = bufa.shape[0]
-    ht = buft.shape[1]
-    ha = bufa.shape[1]
-    a_in = [pltpu.make_async_copy(oact.at[pl.ds(j * ha, ha), :], bufa.at[j], in_a.at[j]) for j in range(na)]
-    a_out = [pltpu.make_async_copy(bufa.at[j], oact_o.at[pl.ds(j * ha, ha), :], out_a.at[j]) for j in range(na)]
-    t_in = [pltpu.make_async_copy(outt.at[pl.ds(j * ht, ht), :], buft.at[j], in_t.at[j]) for j in range(nt)]
-    t_out = [pltpu.make_async_copy(buft.at[j], outt_o.at[pl.ds(j * ht, ht), :], out_t.at[j]) for j in range(nt)]
-    for cp in a_in + t_in:
-        cp.start()
+    homes, C, _, S = ag.shape
+    pltpu.make_async_copy(oact, oact_o, sem.at[0]).start()
+
+    def send(c, carry):
+        for h in range(homes):
+            cols = pl.ds(pl.multiple_of(h * C * S + c * S, S), S)
+            pltpu.make_async_copy(ag.at[h, c], outt_o.at[:, cols], sem.at[1]).start()
+        return carry
+
+    lax.fori_loop(0, C, send, 0)
     for t, (u, w, o) in enumerate(((ug, wg, wg_o), (uu, wu, wu_o), (ud, wd, wd_o))):
         o[...] = w[...] - sv[7:8, t:t + 1] * u[...]
     for t, o in enumerate((rg_o, cg_o, ru_o, cu_o, rd_o, cd_o)):
         o[...] = sv[t:t + 1, :o.shape[1]]
-    for cin, cout in zip(a_in + t_in, a_out + t_out):
-        cin.wait()
-        cout.start()
-    for cp in a_out + t_out:
-        cp.wait()
-
-
-def final_call(outt, oact, ug, uu, ud, sv, wg, wu, wd):
-    m, T = outt.shape
-    ka = oact.shape[1]
+    pltpu.make_async_copy(oact, oact_o, sem.at[0]).wait()
+    pltpu.make_async_copy(outt_o, outt_o, sem.at[1]).wait()
+
+
+def final_call(ag, oact, ug, uu, ud, sv, wg, wu, wd):
+    homes, C, m, S = ag.shape
+    T, ka = oact.shape
     n = ug.shape[1]
     nd = ud.shape[0]
-    nt = m // 16
-    na = 16
-    dma = pltpu.SemaphoreType.DMA
     anyspec = pl.BlockSpec(memory_space=pl.ANY)
     vspec = pl.BlockSpec(memory_space=pltpu.VMEM)
     shape = jax.ShapeDtypeStruct
@@ -621,13 +625,11 @@
             shape((m, n), F32), shape((m, n), F32), shape((nd, ka), F32),
             shape((1, m), F32), shape((1, n), F32), shape((1, m), F32), shape((1, n), F32),
             shape((1, ka), F32), shape((1, nd), F32)),
-        in_specs=[anyspec] * 2 + [vspec] * 7,
+        in_specs=[vspec] * 9,
         out_specs=(anyspec,) * 2 + (vspec,) * 9,
-        scratch_shapes=[
-            pltpu.VMEM((nt, m // nt, T), BF16), pltpu.VMEM((na, T // na, ka), BF16),
-            dma((nt,)), dma((na,)), dma((nt,)), dma((na,))],
-        compiler_params=pltpu.CompilerParams(vmem_limit_bytes=64_000_000),
-    )(outt, oact, ug, uu, ud, sv, wg, wu, wd)
+        scratch_shapes=[pltpu.SemaphoreType.DMA((2,))],
+        compiler_params=pltpu.CompilerParams(vmem_limit_bytes=8_000_000),
+    )(ag, oact, ug, uu, ud, sv, wg, wu, wd)
 
 
 def solution(mesh):
@@ -640,9 +642,10 @@
     def body(w_gate, w_up, w_down, x_norm, x_act, dy_gate, dy_up, dy_down, r_gate, c_gate, r_up, c_up, r_down, c_down, hyper_params):
         wdt = w_down.T
         vecs = [v.reshape(1, -1) for v in (r_gate, c_gate, r_up, c_up, r_down, c_down)]
-        outt, oact, ug, uu, ud, sv = main_call(
+        held = main_call(
             x_norm.T, x_act, dy_gate, dy_up, dy_down.T, w_gate, w_up, wdt, vecs, hyper_params)
-        outt, dx_act, new_gate, new_up, new_down_t, *stats = final_call(outt, oact, ug, uu, ud, sv, w_gate, w_up, wdt)
+        held = [pltpu.with_memory_space_constraint(v, pltpu.VMEM) for v in held]
+        outt, dx_act, new_gate, new_up, new_down_t, *stats = final_call(*held, w_gate, w_up, wdt)
         stats = [v.reshape(-1) for v in stats]
         return (new_gate, new_up, new_down_t.T, *stats, outt.T, dx_act)
 

time: 327 us -> 310 us (0.948)
  Pallas kernels: 325 us -> 308 us
    pallas_call x1, Pallas kernels: 18.1 us -> 8.87 us  [final_call(): pl.pallas_call(final_kernel, out_shape=(shape((m, T), BF16), shape((T, ka...]
    pallas_call x1, Pallas kernels: 307 us -> 299 us  [main_call(): pl.pallas_call(kernel, out_shape=(pltpu.VMEM((NZ, C, m, S), BF16), pltpu....]
where the time goes in v3:
time: 310 us; the launch traced here: 309 us
  Pallas kernels  308 us (99%)
    pallas_call x1, Pallas kernels, main_call(): pl.pallas_call(kernel, out_shape=(pltpu.VMEM((NZ, C, m, S), BF16), pltpu....  299 us
    pallas_call x1, Pallas kernels, final_call(): pl.pallas_call(final_kernel, out_shape=(shape((m, T), BF16), shape((T, ka...  8.87 us

profile of v3, /device:TPU:0, one launch (start us, length us, event | category | flops | bytes accessed | tf_op | source)
XLA Modules:
  0.0 309.0 jit_solution(14760907088715730726)
XLA Ops:
  0.6 0.0 copy-start
  0.7 0.0 copy-start.1
  0.7 0.0 copy-start.2
  0.7 299.4 %shard_map.230 = (bf16[4,32,96,256]{3,2,1,0:T(8,128)(2,1)S(1)}, bf16[32768,256]{1,0:T(8,128)(2,1)S(1)}, f32[96,512]{1,0:T(8,128)S(1)}, f32[96,512]{1,0:T(8,128)S...) custom-call(bf16[96,32768]{1,0:T(8,128)(2,1)} %bitcast.20, bf16[32768,256]{1,0:T(8,128)(2,1)} %xa.1, ...), custom_call_target="tpu_custom_call" | custom-call | tf_op jit(solution)/shard_map/pallas_call | solution.py:572
  300.1 0.0 copy-done
  300.1 0.0 copy-done.1
  300.1 0.0 copy-done.2
  300.1 8.9 %shard_map.231 = (bf16[96,32768]{1,0:T(8,128)(2,1)}, bf16[32768,256]{1,0:T(8,128)(2,1)}, f32[96,512]{1,0:T(8,128)}, f32[96,512]{1,0:T(8,128)}, f32[192,256]{1,0:...) custom-call(bf16[4,32,96,256]{3,2,1,0:T(8,128)(2,1)S(1)} %get-tuple-, ...), custom_call_target="tpu_custom_call" | custom-call | tf_op jit(solution)/shard_map/pallas_call | solution.py:621
Async XLA Ops:
  0.6 299.4 %copy-start = (f32[96,512]{1,0:T(8,128)S(1)}, f32[96,512]{1,0:T(8,128)}, u32[]{:S(2)}) copy-start(f32[96,512]{1,0:T(8,128)} %wg.1) | copy-start | bytes 589828
  0.7 299.4 %copy-start.1 = (f32[96,512]{1,0:T(8,128)S(1)}, f32[96,512]{1,0:T(8,128)}, u32[]{:S(2)}) copy-start(f32[96,512]{1,0:T(8,128)} %wu.1) | copy-start | bytes 589828
  0.7 299.4 %copy-start.2 = (f32[256,192]{0,1:T(8,128)S(1)}, f32[256,192]{0,1:T(8,128)}, u32[]{:S(2)}) copy-start(f32[256,192]{0,1:T(8,128)} %param.17) | copy-start | bytes 589828

commit v4 on v3

--- a/solution.py
+++ b/solution.py
@@ -12,6 +12,9 @@
 NR = 8
 HOME_LAG = (3, 2, 2, 3)
 SKEW = (0, 2, 2, 0)
+UP_AFTER = ((3,), (), (2,), (1,))
+DN_AFTER = ((), (0,), (), (1, 2))
+HOME_AFTER = ((3,), (0,), (2,), (1,))
 AHEAD = 3
 SLOTS = 8
 DRAIN = 6
@@ -32,13 +35,13 @@
 
 
 def kernel(
-    xt, xa, dyg, dyu, dydt, wgf, wuf, wdf, rg, cg, ru, cu, rd, cd, hp,
+    xt, xa, dyg, dyu, dydt, wgh, wuh, wdh, rg, cg, ru, cu, rd, cd, hp,
     ag, oact, gg, gu, gdt, sv,
     rsu, rsd, dz, dxy, wall, part, txt, txa, tg, tu, td, dloc, st,
-    wg, wu, wdt, sa, sb, s1, s2,
+    wg, wu, wdt, sa, sb, s1, s2, wgf, wuf, wdf,
     tile_sem, dloc_sem, rsu_r, rsd_r, ag_r, dz_r, dxy_r, w_r, wp_r,
     rsu_s, rsd_s, agu_s, agd_s, dzu_s, dzd_s, dxy_s, wu_s, wd_s, wp_s,
-    st_s, oact_r, small_s, small_r,
+    st_s, oact_r, small_s, small_r, win_sem,
 ):
     z = lax.axis_index("col")
     i = lax.axis_index("row")
@@ -87,11 +90,9 @@
     me = base + i
     ndev = NZ * NR
 
-    def greet(d, carry):
-        pl.semaphore_signal(barrier, inc=1, device_id=(me + d) % ndev, device_id_type=pl.DeviceIdType.LOGICAL)
-        return carry
-
-    lax.fori_loop(1, ndev, greet, 0)
+    near = [base + q for q in (*plane_peers, partner)] + [((z + d) % NZ) * NR + i for d in (1, NZ - 1)]
+    for dev in near:
+        pl.semaphore_signal(barrier, inc=1, device_id=dev, device_id_type=pl.DeviceIdType.LOGICAL)
 
     def tile_copies(h, c, slot):
         t0 = pl.multiple_of(h * home_len + c * S, S)
@@ -257,6 +258,12 @@
         rms_u = jnp.sqrt(jnp.sum(s2[...], axis=0) / (m_gu * n_gu))
         sv[pl.ds(7, 1), pl.ds(0, 128)] = sv[pl.ds(6, 1), pl.ds(0, 128)] / jnp.maximum(1.0, rms_u / dcut)
 
+    w_in = [
+        pltpu.make_async_copy(src, dst, win_sem.at[t])
+        for t, (src, dst) in enumerate(((wgh, wgf), (wuh, wuf), (wdh, wdf)))
+    ]
+    for cp in w_in:
+        cp.start()
     for t, h in ((0, 3), (1, 0)):
         start_tile(h, 0, t)
     gg[...] = jnp.zeros_like(gg)
@@ -265,11 +272,13 @@
     sa[...] = jnp.zeros_like(sa)
     sb[...] = jnp.zeros_like(sb)
     sv[...] = jnp.zeros_like(sv)
+    for cp in w_in:
+        cp.wait()
     wg[...] = wgf[...].astype(BF16)
     wu[...] = wuf[...].astype(BF16)
     wdt[...] = wdf[...].astype(BF16)
     wall[0, 0] = wdt[...]
-    pl.semaphore_wait(barrier, ndev - 1)
+    pl.semaphore_wait(barrier, len(near))
 
     @pl.when(z < NZ - 1)
     def _():
@@ -363,35 +372,9 @@
                         dn_block(h, c).start()
 
 
-        @pl.when(k == C + 2)
-        def _():
-            first_sums()
-
-        @pl.when(k == C + 4)
-        def _():
-            second_sums()
-
-        order = (3, 0, 2, 1)
-        for t, h in enumerate(order):
-            slot = t % 2
-            kt = k - SKEW[h]
-
-            @pl.when(valid(kt))
-            def _():
-                for cp in tile_copies(h, kt, slot):
-                    cp.wait()
-                g = tg[slot]
-                u = tu[slot]
-                part[kt % 4, h] = mm_nt(wg[...], g) + mm_nt(wu[...], u)
-                gg[...] += mm(txt[slot], g)
-                gu[...] += mm(txt[slot], u)
-                gdt[...] += mm(td[slot], txa[slot])
-
-            hn = order[(t + 2) % 4]
-            start_tile(hn, k + (t + 2) // 4 - SKEW[hn], slot)
-
+        def pass_up(h):
             if h > 0:
-                c = kt - z
+                c = k - SKEW[h] - z
 
                 @pl.when(both(h > z, valid(c)))
                 def _():
@@ -406,8 +389,9 @@
 
                     up_sum(h, c).start()
 
+        def pass_dn(h):
             if h < NZ - 1:
-                c2 = kt - (NZ - 1 - z)
+                c2 = k - SKEW[h] - (NZ - 1 - z)
 
                 @pl.when(both(h < z, valid(c2)))
                 def _():
@@ -422,7 +406,8 @@
 
                     dn_sum(h, c2).start()
 
-            c3 = kt - HOME_LAG[h]
+        def finish(h):
+            c3 = k - SKEW[h] - HOME_LAG[h]
 
             @pl.when(both(h == z, valid(c3)))
             def _():
@@ -438,6 +423,40 @@
                     up_block(h, c3).start()
                 if h > 0:
                     dn_block(h, c3).start()
+
+        order = (3, 0, 2, 1)
+        for t, h in enumerate(order):
+            slot = t % 2
+            kt = k - SKEW[h]
+
+            @pl.when(valid(kt))
+            def _():
+                for cp in tile_copies(h, kt, slot):
+                    cp.wait()
+                g = tg[slot]
+                u = tu[slot]
+                part[kt % 4, h] = mm_nt(wg[...], g) + mm_nt(wu[...], u)
+                gg[...] += mm(txt[slot], g)
+                gu[...] += mm(txt[slot], u)
+                gdt[...] += mm(td[slot], txa[slot])
+
+            hn = order[(t + 2) % 4]
+            start_tile(hn, k + (t + 2) // 4 - SKEW[hn], slot)
+
+            for hu in UP_AFTER[t]:
+                pass_up(hu)
+            for hd in DN_AFTER[t]:
+                pass_dn(hd)
+            for hh in HOME_AFTER[t]:
+                finish(hh)
+
+        @pl.when(k == C + 2)
+        def _():
+            first_sums()
+
+        @pl.when(k == C + 4)
+        def _():
+            second_sums()
 
         @pl.when(k == 3)
         def _():
@@ -564,10 +583,13 @@
         pltpu.VMEM((NZ, 3, 1, 256), F32),
         pltpu.VMEM((NZ * NR, 1, 128), F32),
         pltpu.VMEM((NZ * NR, 1, 128), F32),
+        pltpu.VMEM((m, n), F32),
+        pltpu.VMEM((m, n), F32),
+        pltpu.VMEM((nd, ka), F32),
         dma((2, 5)), dma((2, 4)),
         dma((3, C)), dma((3, C)), dma((NZ, C)), dma((3, C)), dma((3, C)), dma((3,)), dma((1,)),
         dma((3,)), dma((3,)), dma((NZ,)), dma((NZ,)), dma((3,)), dma((3,)), dma((3,)), dma((3,)), dma((3,)), dma((1,)),
-        dma((2, 4)), dma((1,)), dma((4,)), dma((4,)),
+        dma((2, 4)), dma((1,)), dma((4,)), dma((4,)), dma((3,)),
     ]
     return pl.pallas_call(
         kernel,
@@ -579,7 +601,7 @@
             pltpu.VMEM((nd, ka), F32),
             pltpu.VMEM((8, n), F32),
         ),
-        in_specs=[anyspec] * 5 + [vspec] * 9 + [sspec],
+        in_specs=[anyspec] * 8 + [vspec] * 6 + [sspec],
         out_specs=(vspec,) * 6,
         scratch_shapes=scratch,
         compiler_params=pltpu.CompilerParams(

time: 310 us -> 309 us (level)
  no operation moved by 1% of the time
where the time goes in v4:
time: 309 us; the launch traced here: 308 us
  Pallas kernels  307 us (99%)
    pallas_call x1, Pallas kernels, main_call(): pl.pallas_call(kernel, out_shape=(pltpu.VMEM((NZ, C, m, S), BF16), pltpu....  298 us
    pallas_call x1, Pallas kernels, final_call(): pl.pallas_call(final_kernel, out_shape=(shape((m, T), BF16), shape((T, ka...  8.87 us

profile of v4, /device:TPU:0, one launch (start us, length us, event | category | flops | bytes accessed | tf_op | source)
XLA Modules:
  0.0 307.6 jit_solution(4337366017387166934)
XLA Ops:
  0.6 0.0 copy-start
  0.7 0.0 copy-start.1
  0.7 0.0 copy-start.2
  0.7 298.0 %shard_map.230 = (bf16[4,32,96,256]{3,2,1,0:T(8,128)(2,1)S(1)}, bf16[32768,256]{1,0:T(8,128)(2,1)S(1)}, f32[96,512]{1,0:T(8,128)S(1)}, f32[96,512]{1,0:T(8,128)S...) custom-call(bf16[96,32768]{1,0:T(8,128)(2,1)} %bitcast.20, bf16[32768,256]{1,0:T(8,128)(2,1)} %xa.1, ...), custom_call_target="tpu_custom_call" | custom-call | tf_op jit(solution)/shard_map/pallas_call | solution.py:594
  298.7 0.0 copy-done
  298.7 0.0 copy-done.1
  298.7 0.0 copy-done.2
  298.7 8.9 %shard_map.231 = (bf16[96,32768]{1,0:T(8,128)(2,1)}, bf16[32768,256]{1,0:T(8,128)(2,1)}, f32[96,512]{1,0:T(8,128)}, f32[96,512]{1,0:T(8,128)}, f32[192,256]{1,0:...) custom-call(bf16[4,32,96,256]{3,2,1,0:T(8,128)(2,1)S(1)} %get-tuple-, ...), custom_call_target="tpu_custom_call" | custom-call | tf_op jit(solution)/shard_map/pallas_call | solution.py:643
Async XLA Ops:
  0.6 298.0 %copy-start = (f32[96,512]{1,0:T(8,128)S(1)}, f32[96,512]{1,0:T(8,128)}, u32[]{:S(2)}) copy-start(f32[96,512]{1,0:T(8,128)} %wg.1) | copy-start | bytes 589828
  0.7 298.0 %copy-start.1 = (f32[96,512]{1,0:T(8,128)S(1)}, f32[96,512]{1,0:T(8,128)}, u32[]{:S(2)}) copy-start(f32[96,512]{1,0:T(8,128)} %wu.1) | copy-start | bytes 589828
  0.7 298.0 %copy-start.2 = (f32[256,192]{0,1:T(8,128)S(1)}, f32[256,192]{0,1:T(8,128)}, u32[]{:S(2)}) copy-start(f32[256,192]{0,1:T(8,128)} %param.17) | copy-start | bytes 589828
